TPU v7x, 256 devices: a whole 4x4x8 slice. The times are simulated.
256 devices in a mesh: row: 8 (over x, core), col: 32 (over y, z).
Axes of the slice: x: 4, y: 4, z: 8, core: 2. Of those that a mesh axis runs over, the one named last changes fastest.
Arguments:
- basis_raw: float32 [37, 384, 4096], P(None, 'row', 'col'), may hold values from -4 to 4
- krylov_raw: float32 [4, 37, 34], replicated, may hold values from -6 to 6
- stiffness: float32 [384, 4096], P('row', 'col'), may hold values from -0.4 to 0.4
- rotation: float32 [384, 4096], P('row', 'col'), may hold values from -0.2 to 0.2
Outputs:
- new_columns: float32 [3, 384, 4096], P(None, 'row', 'col')
- coefficients: float32 [4, 40, 37], replicated
- hessenberg: float32 [3, 37], replicated
- gram: float32 [5, 40, 5, 40], replicated
- new_images: float32 [3, 384, 4096], P(None, 'row', 'col')
All inputs are finite; a program needn't handle non-finite values.
Results may differ from a plain program's by a relative error of at most 0.001.
Values sent between devices are 32-bit elements; how exact they have to be, the bound alone decides.
A program may use at most 64 MiB of HBM per device.

v0:
```python
import functools
import itertools

import jax
import jax.numpy as jnp
from jax import lax
from jax.experimental import pallas as pl
from jax.experimental.pallas import tpu as pltpu
from jax.sharding import Mesh
from jax.sharding import PartitionSpec as P

K = 40
STEPS = 3
R = 37
KRYLOV = 34
ORDERS = 5
FIELDS = ORDERS * K
COUPLING = 0.2
EPSILON = 1e-06
GRAM_SHIFT = 0.05
HIGHEST = lax.Precision.HIGHEST
AXES = ("x", "core", "y", "z")
ROW = ("x", "core")
COL = ("y", "z")
STAGES = (("x", "core"), ("y",), ("z",))
ROWS = 48
LANES = 128
GHOST = 4
F32 = jnp.float32


def dot(a, b, ca, cb):
    return lax.dot_general(
        a, b, (((ca,), (cb,)), ((), ())), precision=HIGHEST, preferred_element_type=F32
    )


def iota(shape, dim):
    return lax.broadcasted_iota(jnp.int32, shape, dim)


def offsets(sizes, axes):
    ranges = [range(sizes[a]) for a in axes]
    return [o for o in itertools.product(*ranges) if any(o)]


def place(sizes, axes):
    index = 0
    for a in axes:
        index = index * sizes[a] + lax.axis_index(a)
    return index


def peer_of(sizes, axes, off):
    return {a: lax.rem(lax.axis_index(a) + o, sizes[a]) for a, o in zip(axes, off)}


def linear(sizes, axes, coords):
    index = 0
    for a in axes:
        index = index * sizes[a] + coords[a]
    return index


def near(sizes, drow, dcol):
    rows = sizes["x"] * sizes["core"]
    cols = sizes["y"] * sizes["z"]
    r = lax.rem(place(sizes, ROW) + drow + rows, rows)
    c = lax.rem(place(sizes, COL) + dcol + cols, cols)
    return {
        "x": r // sizes["core"],
        "core": lax.rem(r, sizes["core"]),
        "y": c // sizes["z"],
        "z": lax.rem(c, sizes["z"]),
    }


def full(coords):
    return tuple(coords.get(a, lax.axis_index(a)) for a in AXES)


SIDES = [(-1, 0), (1, 0), (0, -1), (0, 1), (-1, -1), (-1, 1), (1, -1), (1, 1)]


def forward_inverse(aug, count):
    sub = iota((K, LANES), 0)
    lane = iota((K, LANES), 1)

    def step(j, a):
        col = jnp.sum(jnp.where(lane == j, a, 0.0), axis=1, keepdims=True)
        row = jnp.sum(jnp.where(sub == j, a, 0.0), axis=0, keepdims=True)
        pivot = jnp.sum(jnp.where(iota((1, LANES), 1) == j, row, 0.0), axis=1, keepdims=True)
        factor = jnp.where(iota((K, 1), 0) > j, col / pivot, 0.0)
        return a - factor * row

    aug = lax.fori_loop(0, count, step, aug)
    diag = jnp.sum(jnp.where(lane == sub, aug, 0.0), axis=1, keepdims=True)
    scaled = aug * (1.0 / jnp.sqrt(diag))
    return jnp.where(lane < K, pltpu.roll(scaled, 64, 1), 0.0)


def augmented(a, shift, count):
    sub = iota((K, LANES), 0)
    lane = iota((K, LANES), 1)
    a = jnp.where((lane < count) & (sub < count), a, 0.0)
    a = a + jnp.where((lane == sub) & (sub < count), shift, 0.0)
    return a + jnp.where(((lane == sub) & (sub >= count)) | (lane == sub + 64), 1.0, 0.0)


def kernel(
    sizes, x_ref, kr_ref, st_ref, ro_ref,
    newc_ref, coef_ref, hess_ref, gram_ref, newi_ref,
    X, SD, T, CF, PL, PR, RRB, RLB, ACC, BIG, FULL, GS, LB, GB0, CB, MT, HS, KS,
    U0, PK, HT, HB, KRB, KLB, VB, DACC,
    slots_big, slots_small,
    hsend, hrecv, bsend, brecv, usend, urecv, ssend, srecv,
):
    nrow = sizes["x"] * sizes["core"]
    ncol = sizes["y"] * sizes["z"]
    my_row = place(sizes, ROW)
    my_col = place(sizes, COL)
    grid_rows = nrow * ROWS
    inverse_total = 1.0 / (grid_rows * ncol * LANES)
    stage_offsets = [offsets(sizes, axes) for axes in STAGES]
    pending = []

    barrier = pltpu.get_barrier_semaphore()
    count = 0
    for axes, offs in zip(STAGES, stage_offsets):
        for off in offs:
            pl.semaphore_signal(
                barrier, inc=1, device_id=full(peer_of(sizes, axes, off)),
                device_id_type=pl.DeviceIdType.MESH,
            )
            count += 1
    for side in SIDES:
        pl.semaphore_signal(
            barrier, inc=1, device_id=full(near(sizes, *side)),
            device_id_type=pl.DeviceIdType.MESH,
        )
        count += 1

    def send(src, dst, ssem, rsem, coords):
        copy = pltpu.make_async_remote_copy(
            src_ref=src, dst_ref=dst, send_sem=ssem, recv_sem=rsem,
            device_id=full(coords), device_id_type=pl.DeviceIdType.MESH,
        )
        copy.start()
        pending.append(copy)
        return copy

    def load_row(r, carry):
        X[0, r + GHOST, pl.ds(0, R), :] = x_ref[pl.ds(r, R, stride=ROWS), :]
        X[0, r + GHOST, pl.ds(R, 1), :] = st_ref[pl.ds(r, 1), :]
        X[0, r + GHOST, pl.ds(R + 1, 1), :] = ro_ref[pl.ds(r, 1), :]
        X[0, r + GHOST, pl.ds(R + 2, 1), :] = jnp.zeros((1, LANES), F32)
        return carry

    lax.fori_loop(0, ROWS, load_row, 0)
    lane_k = iota((K, LANES), 1)

    def pack(base, n, q):
        def body(i, carry):
            left, right = carry
            row = X[0, base + i, :, :]
            here = (lane_k >= 4 * i) & (lane_k < 4 * i + 4)
            left = jnp.where(here, pltpu.roll(row, 4 * i, 1), left)
            right = jnp.where(here, pltpu.roll(row, lax.rem(4 * i + 4, LANES), 1), right)
            return left, right

        zero = jnp.zeros((K, LANES), F32)
        left, right = lax.fori_loop(0, n, body, (zero, zero))
        PL[q, :, :] = left
        PR[q, :, :] = right

    pack(GHOST, 32, 0)
    pack(GHOST + 32, 16, 1)
    pl.semaphore_wait(barrier, count)

    halo = [
        send(X.at[0, pl.ds(GHOST, GHOST)], X.at[0, pl.ds(GHOST + ROWS, GHOST)], hsend.at[0], hrecv.at[0], near(sizes, -1, 0)),
        send(X.at[0, pl.ds(ROWS, GHOST)], X.at[0, pl.ds(0, GHOST)], hsend.at[1], hrecv.at[1], near(sizes, 1, 0)),
        send(PL, RRB.at[pl.ds(1, 2)], hsend.at[2], hrecv.at[2], near(sizes, 0, -1)),
        send(PR, RLB.at[pl.ds(1, 2)], hsend.at[3], hrecv.at[3], near(sizes, 0, 1)),
        send(PL.at[0], RRB.at[3], hsend.at[4], hrecv.at[4], near(sizes, -1, -1)),
        send(PR.at[0], RLB.at[3], hsend.at[5], hrecv.at[5], near(sizes, -1, 1)),
        send(PL.at[1], RRB.at[0], hsend.at[6], hrecv.at[6], near(sizes, 1, -1)),
        send(PR.at[1], RLB.at[0], hsend.at[7], hrecv.at[7], near(sizes, 1, 1)),
    ]

    KS[...] = jnp.zeros((256, LANES), F32)
    for j in range(4):
        KS[pl.ds(j * K, R), pl.ds(0, KRYLOV)] = kr_ref[j]
    pt = jnp.transpose(KS[...])[0:K, :]
    kgram = dot(pt, KS[...], 1, 0)
    kinv = forward_inverse(augmented(kgram, 0.0, KRYLOV), KRYLOV)
    MT[...] = jnp.zeros((LANES, 256), F32)
    MT[pl.ds(0, K), :] = dot(kinv[:, 0:K], pt, 1, 0)
    HS[...] = jnp.zeros((LANES, LANES), F32)
    LB[...] = jnp.zeros((256, 256), F32)
    GS[...] = jnp.zeros((256, 256), F32)
    BIG[...] = jnp.zeros((256, LANES), F32)
    CF[...] = jnp.zeros((10, 64, LANES), F32)
    for m in range(ORDERS):
        DACC[m, pl.ds(FIELDS, 56), :] = jnp.zeros((56, LANES), F32)

    for copy in halo:
        copy.wait_recv()
    for copy in halo[:2]:
        copy.wait_send()
        pending.remove(copy)

    lane1 = iota((1, LANES), 1)
    has_right = (my_col < ncol - 1).astype(F32)
    has_left = (my_col > 0).astype(F32)
    side_mask = jnp.where(lane1 < 4, has_right, jnp.where(lane1 >= 124, has_left, 0.0))
    sub_k = iota((K, LANES), 0)

    def order_zero(base, n, part, first):
        def body(i, carry):
            rho = base + i
            g = my_row * ROWS + rho - GHOST
            row_mask = ((g >= 0) & (g < grid_rows)).astype(F32)
            at = 4 * (first + i)
            right = pltpu.roll(RRB[part, :, :], lax.rem(LANES - at, LANES), 1)
            left = pltpu.roll(RLB[part, :, :], lax.rem(2 * LANES - 4 - at, LANES), 1)
            ms = side_mask * row_mask
            side = jnp.where(lane_k < 4, right, left) * ms
            mid = X[0, rho, :, :] * row_mask
            mc = jnp.ones((1, LANES), F32) * row_mask
            for half, (v, m) in enumerate(((mid, mc), (side, ms))):
                d = v[R : R + 1, :]
                s = v[R + 1 : R + 2, :]
                CF[5 * half, pl.ds(rho + 4, 1), :] = 2.0 * d * m
                CF[5 * half + 1, pl.ds(rho + 4, 1), :] = (2.0 * COUPLING) * m
                CF[5 * half + 2, pl.ds(rho + 4, 1), :] = 2.0 * (s - COUPLING) * m
                CF[5 * half + 3, pl.ds(rho + 4, 1), :] = 2.0 * (s + COUPLING) * m
                CF[5 * half + 4, pl.ds(rho + 4, 1), :] = m
            X[0, rho, :, :] = jnp.where(sub_k < R, mid, 0.0)
            SD[0, rho, :, :] = jnp.where(sub_k < R, side, 0.0)
            return carry

        lax.fori_loop(0, n, body, 0)

    order_zero(0, 4, 0, 12)
    order_zero(4, 32, 1, 0)
    order_zero(36, 16, 2, 0)
    order_zero(52, 4, 3, 0)

    def copy_zero(r, carry):
        T[pl.ds(pl.multiple_of(r * FIELDS, 8), K), :] = X[0, r + GHOST, :, :]
        return carry

    lax.fori_loop(0, ROWS, copy_zero, 0)

    def images(m):
        def body(i, carry):
            rho = m + i
            c = X[m - 1, rho, :, :]
            s = SD[m - 1, rho, :, :]
            cu = X[m - 1, rho - 1, :, :] + X[m - 1, rho + 1, :, :]
            cl, sl = pltpu.roll(c, 1, 1), pltpu.roll(s, 1, 1)
            cr, sr = pltpu.roll(c, 127, 1), pltpu.roll(s, 127, 1)

            def row(kind):
                return CF[kind, pl.ds(rho + 4, 1), :]

            left = jnp.where(lane_k == 0, sl, cl)
            right = jnp.where(lane_k == 127, sr, cr)
            new = row(0) * c - row(1) * cu + row(2) * right - row(3) * left
            new = 0.5 * new if m == 1 else new - X[m - 2, rho, :, :]
            if m < 4:
                X[m, rho, :, :] = new
                su = SD[m - 1, rho - 1, :, :] + SD[m - 1, rho + 1, :, :]
                left = jnp.where(lane_k == 0, cl, sl)
                right = jnp.where(lane_k == 127, cr, sr)
                side = row(5) * s - row(6) * su + row(7) * right - row(8) * left
                SD[m, rho, :, :] = 0.5 * side if m == 1 else side - SD[m - 2, rho, :, :]

                @pl.when((rho >= GHOST) & (rho < GHOST + ROWS))
                def _():
                    at = pl.multiple_of((rho - GHOST) * FIELDS + m * K, 8)
                    T[pl.ds(at, K), :] = new
            else:
                at = pl.multiple_of((rho - GHOST) * FIELDS + m * K, 8)
                T[pl.ds(at, K), :] = new
            return carry

        lax.fori_loop(0, ROWS + 8 - 2 * m, body, 0)

    for m in range(1, ORDERS):
        images(m)

    ACC[...] = jnp.zeros((FIELDS, 256), F32)

    def gram_rows(g, carry):
        a = jnp.concatenate(
            [T[pl.ds(pl.multiple_of((4 * g + k) * FIELDS, 8), FIELDS), :] for k in range(4)], axis=1
        )
        ACC[:, pl.ds(0, FIELDS)] += dot(a, a, 1, 1)
        return carry

    lax.fori_loop(0, ROWS // 4, gram_rows, 0)

    def strip(ref, a, shift):
        v = ref[pl.ds(a * K, K), :]
        return pltpu.roll(v, shift % 256, 1) if shift % 256 else v

    lane_n = iota((K, LANES), 1)
    last = lane_n >= 80
    BIG[pl.ds(0, K), :] = strip(ACC, 0, 0)[:, 0:LANES]
    BIG[pl.ds(K, K), :] = strip(ACC, 1, -40)[:, 0:LANES]
    BIG[pl.ds(2 * K, K), :] = strip(ACC, 2, -80)[:, 0:LANES]
    BIG[pl.ds(3 * K, K), :] = jnp.where(last, strip(ACC, 4, -80)[:, 0:LANES], strip(ACC, 0, -120)[:, 0:LANES])
    BIG[pl.ds(4 * K, K), :] = jnp.where(last, strip(ACC, 1, -80)[:, 0:LANES], strip(ACC, 3, -120)[:, 0:LANES])

    chunk = 256 // nrow
    own = pl.ds(pl.multiple_of(my_row * chunk, 8), chunk)

    def chunk_of(coords):
        return pl.ds(pl.multiple_of(linear(sizes, ROW, coords) * chunk, 8), chunk)

    sem = 0
    for stage, (axes, offs) in enumerate(zip(STAGES, stage_offsets)):
        me = place(sizes, axes)
        box = slots_big[stage]
        if stage == 0:
            box[me] = BIG[own, :]
        copies = []
        for off in offs:
            to = peer_of(sizes, axes, off)
            src = BIG.at[chunk_of(to)] if stage == 0 else box.at[me]
            copies.append(send(src, box.at[me], bsend.at[sem], brecv.at[sem], to))
            sem += 1
        for copy in copies:
            copy.wait_recv()
        total = box[0]
        for i in range(1, len(offs) + 1):
            total = total + box[i]
        if stage + 1 < len(STAGES):
            slots_big[stage + 1][place(sizes, STAGES[stage + 1])] = total
        else:
            FULL[own, :] = total * inverse_total
    copies = []
    for off in stage_offsets[0]:
        to = peer_of(sizes, ROW, off)
        copies.append(send(FULL.at[own], FULL.at[own], bsend.at[sem], brecv.at[sem], to))
        sem += 1
    for copy in copies:
        copy.wait_recv()

    lane_w = iota((K, 256), 1)

    def wide(a):
        v = FULL[pl.ds(a * K, K), :]
        return jnp.concatenate([jnp.where(lane_n < 120, v, 0.0), jnp.zeros((K, LANES), F32)], axis=1)

    g3, g4 = wide(3), wide(4)

    def between(v, lo, hi):
        return jnp.where((lane_w >= lo) & (lane_w < hi), v, 0.0)

    GS[pl.ds(0, K), :] = wide(0) + between(pltpu.roll(g3, 120, 1), 120, 200)
    GS[pl.ds(K, K), :] = pltpu.roll(wide(1), 40, 1) + between(pltpu.roll(g4, 80, 1), 160, 200)
    GS[pl.ds(2 * K, K), :] = pltpu.roll(wide(2), 80, 1)
    GS[pl.ds(3 * K, K), :] = between(pltpu.roll(g4, 120, 1), 120, 200)
    GS[pl.ds(4 * K, K), :] = between(pltpu.roll(g3, 80, 1), 160, 200)
    mirrored = jnp.transpose(GS[...])
    for a in range(1, ORDERS):
        GS[pl.ds(a * K, K), :] = jnp.where(
            lane_w >= a * K, GS[pl.ds(a * K, K), :], mirrored[a * K : (a + 1) * K, :]
        )

    finv = forward_inverse(augmented(GS[pl.ds(0, K), pl.ds(0, LANES)], GRAM_SHIFT, R), R)
    finv = jnp.where(sub_k < R, finv, 0.0)
    finv_wide = jnp.concatenate([finv, jnp.zeros((K, LANES), F32)], axis=1)
    for a in range(ORDERS):
        LB[pl.ds(a * K, K), :] = pltpu.roll(finv_wide, a * K, 1) if a else finv_wide
    square = (iota((LANES, LANES), 0) < K) & (iota((LANES, LANES), 1) < K)
    small = jnp.where(square, LB[pl.ds(0, LANES), pl.ds(0, LANES)], 0.0)
    GB0[...] = dot(dot(LB[...], GS[:, pl.ds(0, LANES)], 1, 0), small, 1, 1)

    lane_r = iota((1, 256), 1)
    lane8 = iota((8, 256), 1)
    sub8 = iota((8, 256), 0)
    tile_mask = iota((64, LANES), 1)

    for s in range(STEPS):
        column = KRYLOV + s
        r = R + s
        latest = MT[pl.ds(column - 1, 1), :]

        def moved(shift):
            return pltpu.roll(latest, shift % 256, 1)

        cw = jnp.where(lane_r < K, 0.5 * moved(-80), -0.5 * moved(40))
        cw = jnp.where(lane_r < FIELDS, cw, 0.0)
        cw = jnp.broadcast_to(cw, (8, 256))
        h1 = dot(cw, GB0[...], 1, 0)
        h = 2.0 * h1 - dot(h1, GB0[pl.ds(0, LANES), :], 1, 0)
        h_wide = jnp.concatenate([h, jnp.zeros((8, LANES), F32)], axis=1)
        raw = dot(cw - h_wide, LB[...], 1, 0)
        raw_col = jnp.transpose(raw)[0:FIELDS, 0:1]
        CB[...] = jnp.broadcast_to(raw_col, (FIELDS, LANES))

        def combine(i, carry):
            for k in range(8):
                at = pl.multiple_of((8 * i + k) * FIELDS, 8)
                value = jnp.sum(CB[...] * T[pl.ds(at, FIELDS), :], axis=0, keepdims=True)
                U0[s, pl.ds(8 * i + k, 1), :] = value
            return carry

        lax.fori_loop(0, ROWS // 8, combine, 0)

        lane_t = iota((8, LANES), 1)
        packed = jnp.zeros((8, LANES), F32)
        for q in range(6):
            tile = U0[s, pl.ds(8 * q, 8), :]
            packed = jnp.where(
                (lane_t >= 4 * q) & (lane_t < 4 * q + 4), pltpu.roll(tile, 4 * q, 1) if q else tile, packed
            )
            packed = jnp.where(
                (lane_t >= 64 + 4 * q) & (lane_t < 68 + 4 * q), pltpu.roll(tile, 68 + 4 * q, 1), packed
            )
        PK[s, :, :] = packed
        edge = [
            send(U0.at[s, pl.ds(0, 8)], HB.at[s], usend.at[s, 0], urecv.at[s, 0], near(sizes, -1, 0)),
            send(U0.at[s, pl.ds(40, 8)], HT.at[s], usend.at[s, 1], urecv.at[s, 1], near(sizes, 1, 0)),
            send(PK.at[s], KRB.at[s, 1], usend.at[s, 2], urecv.at[s, 2], near(sizes, 0, -1)),
            send(PK.at[s], KLB.at[s, 1], usend.at[s, 3], urecv.at[s, 3], near(sizes, 0, 1)),
            send(PK.at[s], KRB.at[s, 2], usend.at[s, 4], urecv.at[s, 4], near(sizes, -1, -1)),
            send(PK.at[s], KLB.at[s, 2], usend.at[s, 5], urecv.at[s, 5], near(sizes, -1, 1)),
            send(PK.at[s], KRB.at[s, 0], usend.at[s, 6], urecv.at[s, 6], near(sizes, 1, -1)),
            send(PK.at[s], KLB.at[s, 0], usend.at[s, 7], urecv.at[s, 7], near(sizes, 1, 1)),
        ]

        h_row = h_wide[0:1, :]
        e = jnp.where(lane_r < K, moved(-40), 0.5 * (moved(40) + moved(-40)))
        e = jnp.where(lane_r < 3 * K, e, pltpu.roll(h_row, 3 * K, 1))
        e = jnp.where(lane_r < 4 * K, e, 0.0)
        mt = MT[pl.ds(0, K), :]
        g1 = jnp.sum(mt * e, axis=1, keepdims=True)
        e1 = e - jnp.sum(mt * g1, axis=0, keepdims=True)
        g2 = jnp.sum(mt * e1, axis=1, keepdims=True)
        e2 = e1 - jnp.sum(mt * g2, axis=0, keepdims=True)
        e2_square = jnp.sum(e2 * e2, axis=1, keepdims=True)

        for copy in edge:
            copy.wait_recv()

        mids = jnp.concatenate([HT[s], U0[s], HB[s]], axis=0) * CF[4]
        sides = []
        for j in range(8):
            part = 0 if j == 0 else (2 if j == 7 else 1)
            q = 5 if j == 0 else (0 if j == 7 else j - 1)
            rt = KRB[s, part]
            lf = pltpu.roll(KLB[s, part], 60 - 4 * q, 1)
            rt = pltpu.roll(rt, LANES - 4 * q, 1) if q else rt
            sides.append(jnp.where(lane_t < 4, rt, lf))
        sds = jnp.concatenate(sides, axis=0) * CF[9]

        def twice_s(c, v):
            cl, sl = pltpu.roll(c, 1, 1), pltpu.roll(v, 1, 1)
            cr, sr = pltpu.roll(c, 127, 1), pltpu.roll(v, 127, 1)
            cu = pltpu.roll(c, 1, 0) + pltpu.roll(c, 63, 0)
            su = pltpu.roll(v, 1, 0) + pltpu.roll(v, 63, 0)
            lo, hi = tile_mask == 0, tile_mask == 127
            mid = CF[0] * c - CF[1] * cu + CF[2] * jnp.where(hi, sr, cr) - CF[3] * jnp.where(lo, sl, cl)
            side = CF[5] * v - CF[6] * su + CF[7] * jnp.where(hi, cr, sr) - CF[8] * jnp.where(lo, cl, sl)
            return mid, side

        before = (mids, sds)
        now = twice_s(*before)
        now = (0.5 * now[0], 0.5 * now[1])
        orders = [before[0], now[0]]
        for m in range(2, ORDERS):
            nxt = twice_s(*now)
            before, now = now, (nxt[0] - before[0], nxt[1] - before[1])
            orders.append(now[0])
        for m in range(ORDERS):
            VB[m, :, :] = orders[m][8:56, :]
            T[pl.ds(m * K + r, ROWS, stride=FIELDS), :] = orders[m][8:56, :]

        for a in range(ORDERS):
            def products(i, accs):
                at = pl.multiple_of(i * FIELDS + a * K, 8)
                t = T[pl.ds(at, K), :]
                return tuple(acc + t * VB[m, pl.ds(i, 1), :] for m, acc in enumerate(accs))

            accs = lax.fori_loop(
                0, ROWS, products, tuple(jnp.zeros((K, LANES), F32) for _ in range(ORDERS))
            )
            for m in range(ORDERS):
                DACC[m, pl.ds(a * K, K), :] = accs[m]
        d = jnp.zeros((8, 256), F32)
        for m in range(ORDERS):
            pick = (iota((8, LANES), 0) == m).astype(F32)
            d = d + dot(pick, DACC[m], 1, 1)

        total = d
        sem = 0
        for stage, (axes, offs) in enumerate(zip(STAGES, stage_offsets)):
            me = place(sizes, axes)
            box = slots_small[stage].at[s]
            box[me] = total
            copies = []
            for off in offs:
                copies.append(
                    send(box.at[me], box.at[me], ssend.at[s, sem], srecv.at[s, sem], peer_of(sizes, axes, off))
                )
                sem += 1
            for copy in copies:
                copy.wait_recv()
            total = box[0]
            for i in range(1, len(offs) + 1):
                total = total + box[i]
        d = total * inverse_total

        nn = jnp.sum(jnp.where(lane_r == r, d[0:1, :], 0.0), axis=1, keepdims=True)
        beta = jnp.sqrt(nn + EPSILON)
        ib = 1.0 / beta
        eta = jnp.sqrt(e2_square + beta * beta + EPSILON)
        MT[pl.ds(column, 1), :] = (e2 + jnp.where(lane_r == 3 * K + r, beta, 0.0)) / eta
        sub_col = iota((K, 1), 0)
        g = g1 + g2 + jnp.where(sub_col == column, eta, 0.0)
        lane_h = iota((K, LANES), 1)
        HS[pl.ds(0, K), :] = jnp.where(lane_h == s, g, HS[pl.ds(0, K), :])
        newc_ref[s, :, :] = VB[0] * ib
        newi_ref[s, :, :] = VB[4] * ib
        for m in range(ORDERS):
            at = m * K + r
            LB[pl.ds(at, 1), :] = jnp.where(lane_r == at, ib, 0.0)
            GS[pl.ds(at, 1), :] = d[m : m + 1, :]
        if s + 1 < STEPS:
            db = dot(d, LB[...], 1, 1) * ib
            dcol = jnp.transpose(db)[:, 0:1]
            lane_g = iota((256, LANES), 1)
            GB0[...] = jnp.where(lane_g == r, dcol, GB0[...])
            for m in range(ORDERS):
                GB0[pl.ds(m * K + r, 1), :] = jnp.where(lane1 < K, db[m : m + 1, 0:LANES], 0.0)

    mirrored = jnp.transpose(GS[...])
    field = lane_w
    for a in range(1, ORDERS):
        field = field - jnp.where(lane_w >= a * K, K, 0)
    age_col = jnp.maximum(field - (R - 1), 0)
    age_row = jnp.maximum(iota((K, 256), 0) - (R - 1), 0)
    for a in range(ORDERS):
        GS[pl.ds(a * K, K), :] = jnp.where(
            age_row >= age_col, GS[pl.ds(a * K, K), :], mirrored[a * K : (a + 1) * K, :]
        )
    gram = dot(dot(LB[...], GS[...], 1, 0), LB[...], 1, 1)
    gram_ref[...] = gram[0:FIELDS, 0:FIELDS]
    mcol = jnp.transpose(MT[...])
    for j in range(4):
        coef_ref[j, :, :] = mcol[j * K : (j + 1) * K, 0 : KRYLOV + STEPS]
    hess_ref[...] = jnp.transpose(HS[...])[0:STEPS, 0 : KRYLOV + STEPS]

    for copy in pending:
        copy.wait_send()


def local(sizes, basis_raw, krylov_raw, stiffness, rotation):
    width = KRYLOV + STEPS
    nrow = sizes["x"] * sizes["core"]
    counts = []
    for axes in STAGES:
        n = 1
        for a in axes:
            n *= sizes[a]
        counts.append(n)
    chunk = 256 // nrow
    big_copies = sum(n - 1 for n in counts) + counts[0] - 1
    small_copies = sum(n - 1 for n in counts)
    vmem = lambda *shape: pltpu.VMEM(shape, F32)
    dma = lambda *shape: pltpu.SemaphoreType.DMA(shape)
    scratch = [
        vmem(4, ROWS + 8, K, LANES), vmem(4, ROWS + 8, K, LANES), vmem(ROWS * FIELDS, LANES),
        vmem(10, 64, LANES), vmem(2, K, LANES), vmem(2, K, LANES), vmem(4, K, LANES), vmem(4, K, LANES),
        vmem(FIELDS, 256), vmem(256, LANES), vmem(256, LANES), vmem(256, 256), vmem(256, 256),
        vmem(256, LANES), vmem(FIELDS, LANES), vmem(LANES, 256), vmem(LANES, LANES), vmem(256, LANES),
        vmem(STEPS, ROWS, LANES), vmem(STEPS, 8, LANES), vmem(STEPS, 8, LANES), vmem(STEPS, 8, LANES),
        vmem(STEPS, 3, 8, LANES), vmem(STEPS, 3, 8, LANES), vmem(ORDERS, ROWS, LANES),
        vmem(ORDERS, 256, LANES),
        [vmem(n, chunk, LANES) for n in counts],
        [vmem(STEPS, n, 8, 256) for n in counts],
        dma(8), dma(8), dma(big_copies), dma(big_copies),
        dma(STEPS, 8), dma(STEPS, 8), dma(STEPS, small_copies), dma(STEPS, small_copies),
    ]
    shape = lambda *dims: jax.ShapeDtypeStruct(dims, F32)
    new_columns, coefficients, hessenberg, gram, new_images = pl.pallas_call(
        functools.partial(kernel, sizes),
        out_shape=[
            shape(STEPS, ROWS, LANES), shape(4, K, width), shape(STEPS, width),
            shape(FIELDS, FIELDS), shape(STEPS, ROWS, LANES),
        ],
        in_specs=[pl.BlockSpec(memory_space=pltpu.VMEM)] * 4,
        out_specs=[pl.BlockSpec(memory_space=pltpu.VMEM)] * 5,
        scratch_shapes=scratch,
        compiler_params=pltpu.CompilerParams(
            collective_id=0, has_side_effects=True, vmem_limit_bytes=48 * 1024 * 1024
        ),
    )(basis_raw.reshape(R * ROWS, LANES), krylov_raw, stiffness, rotation)
    return new_columns, coefficients, hessenberg, gram.reshape(ORDERS, K, ORDERS, K), new_images


def solution(mesh):
    cores = 2
    columns = mesh.devices.shape[1]
    depth = 8 if columns % 8 == 0 else 2
    sizes = {
        "x": mesh.devices.shape[0] // cores, "core": cores,
        "y": columns // depth, "z": depth,
    }
    split = Mesh(mesh.devices.reshape(*(sizes[a] for a in AXES)), AXES)
    return jax.shard_map(
        functools.partial(local, sizes),
        mesh=split,
        in_specs=(P(None, ROW, COL), P(), P(ROW, COL), P(ROW, COL)),
        out_specs=(P(None, ROW, COL), P(), P(), P(), P(None, ROW, COL)),
        check_vma=False,
    )
```

profile of v0, /device:TPU:2, one launch (start us, length us, event | category | flops | bytes accessed | tf_op | source)
XLA Modules:
  0.0 144.9 jit_solution(15217935683066804253)
XLA Ops:
  0.6 0.0 copy-start.1
  0.6 0.0 copy-start.2
  0.7 1.0 copy.12.kr_ref
  1.7 0.0 copy-done.1
  1.7 0.0 copy-done.2
  1.7 0.0 copy-start
  1.7 1.2 copy-done
  2.8 138.4 %shard_map.83 = (f32[3,48,128]{2,1,0:T(8,128)S(1)}, f32[4,40,37]{2,1,0:T(8,128)S(1)}, f32[3,37]{1,0:T(4,128)S(1)}, f32[200,200]{1,0:T(8,128)S(1)}, f32[3,48,128]{2,1,0:T(8,128)S(1)}) custom-call(f32[1776,128]{1,0:T(8,128)S(1)} %bitcast.1, f32[4,37,34]{2,1,0:T(8,128)S(1)} %copy.12.kr_ref, f32[48,128]{1,0:T(8,128)S(1)} %copy-done.1, f32[48,128]{1,0:T(8,128)S(1)} %copy-done.2), custom_call_target="tpu_custom_call" | custom-call | tf_op jit(solution)/shard_map/pallas_call | solution.py:591
  141.2 0.7 copy.13
  142.0 0.2 reshape.17
  142.2 0.9 copy.14
  143.0 0.6 copy.18
  143.7 0.6 copy.19
  144.2 0.6 copy.20
Async XLA Ops:
  0.6 1.0 copy-start.1
  0.6 1.0 copy-start.2
  1.7 1.2 copy-start
where the time goes:
time: 145 us
  Pallas kernels  138 us (95%)
  local copies, waits for them, and re-layouts  5.84 us (4%)
    pallas_call x1, Pallas kernels, local(): pl.pallas_call(functools.partial(kernel, sizes), out_shape=[shape(STEPS,...  138 us
    unnamed x12, local copies, waits for them, and re-layouts  5.64 us

commit v1 on v0

--- a/solution.py
+++ b/solution.py
@@ -26,6 +26,8 @@
 ROWS = 48
 LANES = 128
 GHOST = 4
+PADDED = 208
+GROUP = 8
 F32 = jnp.float32
 
 
@@ -82,20 +84,22 @@
 SIDES = [(-1, 0), (1, 0), (0, -1), (0, 1), (-1, -1), (-1, 1), (1, -1), (1, 1)]
 
 
-def forward_inverse(aug, count):
+def forward_inverse(a, count, block=4):
     sub = iota((K, LANES), 0)
     lane = iota((K, LANES), 1)
-
-    def step(j, a):
-        col = jnp.sum(jnp.where(lane == j, a, 0.0), axis=1, keepdims=True)
-        row = jnp.sum(jnp.where(sub == j, a, 0.0), axis=0, keepdims=True)
-        pivot = jnp.sum(jnp.where(iota((1, LANES), 1) == j, row, 0.0), axis=1, keepdims=True)
-        factor = jnp.where(iota((K, 1), 0) > j, col / pivot, 0.0)
-        return a - factor * row
-
-    aug = lax.fori_loop(0, count, step, aug)
-    diag = jnp.sum(jnp.where(lane == sub, aug, 0.0), axis=1, keepdims=True)
-    scaled = aug * (1.0 / jnp.sqrt(diag))
+    for first in range(0, count, block):
+        pivots = range(first, min(first + block, count))
+        cols = [jnp.broadcast_to(a[:, j : j + 1], (K, LANES)) for j in pivots]
+        rows = [a[j : j + 1, :] for j in pivots]
+        for p, j in enumerate(pivots):
+            inverse = 1.0 / cols[p][j : j + 1, :]
+            factor = jnp.where(sub > j, cols[p] * inverse, 0.0)
+            for q in range(p + 1, len(pivots)):
+                cols[q] = cols[q] - factor * cols[q][j : j + 1, :]
+                rows[q] = rows[q] - factor[pivots[q] : pivots[q] + 1, :] * rows[p]
+            a = a - factor * rows[p]
+    diag = jnp.sum(jnp.where(lane == sub, a, 0.0), axis=1, keepdims=True)
+    scaled = a * (1.0 / jnp.sqrt(diag))
     return jnp.where(lane < K, pltpu.roll(scaled, 64, 1), 0.0)
 
 
@@ -110,8 +114,8 @@
 def kernel(
     sizes, x_ref, kr_ref, st_ref, ro_ref,
     newc_ref, coef_ref, hess_ref, gram_ref, newi_ref,
-    X, SD, T, CF, PL, PR, RRB, RLB, ACC, BIG, FULL, GS, LB, GB0, CB, MT, HS, KS,
-    U0, PK, HT, HB, KRB, KLB, VB, DACC,
+    X, SD, CF, PL, PR, RRB, RLB, AHL, ACC, BIG, FULL, GS, LB, GB0, CB, MT, HS, KS,
+    U0, PK, HT, HB, KRB, KLB, VB, VW, UV, DN,
     slots_big, slots_small,
     hsend, hrecv, bsend, brecv, usend, urecv, ssend, srecv,
 ):
@@ -149,27 +153,35 @@
         pending.append(copy)
         return copy
 
-    def load_row(r, carry):
-        X[0, r + GHOST, pl.ds(0, R), :] = x_ref[pl.ds(r, R, stride=ROWS), :]
-        X[0, r + GHOST, pl.ds(R, 1), :] = st_ref[pl.ds(r, 1), :]
-        X[0, r + GHOST, pl.ds(R + 1, 1), :] = ro_ref[pl.ds(r, 1), :]
-        X[0, r + GHOST, pl.ds(R + 2, 1), :] = jnp.zeros((1, LANES), F32)
+    def load_rows(i, carry):
+        for k in range(4):
+            r = 4 * i + k
+            at = pl.multiple_of((r + GHOST) * K, 8)
+            X[0][pl.ds(at, R), :] = x_ref[pl.ds(r, R, stride=ROWS), :]
+            X[0][pl.ds(at + R, 1), :] = st_ref[pl.ds(r, 1), :]
+            X[0][pl.ds(at + R + 1, 1), :] = ro_ref[pl.ds(r, 1), :]
+            X[0][pl.ds(at + R + 2, 1), :] = jnp.zeros((1, LANES), F32)
         return carry
 
-    lax.fori_loop(0, ROWS, load_row, 0)
+    lax.fori_loop(0, ROWS // 4, load_rows, 0)
     lane_k = iota((K, LANES), 1)
 
+    def line(rho):
+        return pl.ds(pl.multiple_of(rho * K, 8), K)
+
     def pack(base, n, q):
-        def body(i, carry):
+        def body(b, carry):
             left, right = carry
-            row = X[0, base + i, :, :]
-            here = (lane_k >= 4 * i) & (lane_k < 4 * i + 4)
-            left = jnp.where(here, pltpu.roll(row, 4 * i, 1), left)
-            right = jnp.where(here, pltpu.roll(row, lax.rem(4 * i + 4, LANES), 1), right)
+            for k in range(8):
+                i = 8 * b + k
+                row = X[0][line(base + i), :]
+                here = (lane_k >= 4 * i) & (lane_k < 4 * i + 4)
+                left = jnp.where(here, pltpu.roll(row, 4 * i, 1), left)
+                right = jnp.where(here, pltpu.roll(row, lax.rem(4 * i + 4, LANES), 1), right)
             return left, right
 
         zero = jnp.zeros((K, LANES), F32)
-        left, right = lax.fori_loop(0, n, body, (zero, zero))
+        left, right = lax.fori_loop(0, n // 8, body, (zero, zero))
         PL[q, :, :] = left
         PR[q, :, :] = right
 
@@ -178,8 +190,8 @@
     pl.semaphore_wait(barrier, count)
 
     halo = [
-        send(X.at[0, pl.ds(GHOST, GHOST)], X.at[0, pl.ds(GHOST + ROWS, GHOST)], hsend.at[0], hrecv.at[0], near(sizes, -1, 0)),
-        send(X.at[0, pl.ds(ROWS, GHOST)], X.at[0, pl.ds(0, GHOST)], hsend.at[1], hrecv.at[1], near(sizes, 1, 0)),
+        send(X[0].at[pl.ds(GHOST * K, GHOST * K)], X[0].at[pl.ds((GHOST + ROWS) * K, GHOST * K)], hsend.at[0], hrecv.at[0], near(sizes, -1, 0)),
+        send(X[0].at[pl.ds(ROWS * K, GHOST * K)], X[0].at[pl.ds(0, GHOST * K)], hsend.at[1], hrecv.at[1], near(sizes, 1, 0)),
         send(PL, RRB.at[pl.ds(1, 2)], hsend.at[2], hrecv.at[2], near(sizes, 0, -1)),
         send(PR, RLB.at[pl.ds(1, 2)], hsend.at[3], hrecv.at[3], near(sizes, 0, 1)),
         send(PL.at[0], RRB.at[3], hsend.at[4], hrecv.at[4], near(sizes, -1, -1)),
@@ -201,8 +213,8 @@
     GS[...] = jnp.zeros((256, 256), F32)
     BIG[...] = jnp.zeros((256, LANES), F32)
     CF[...] = jnp.zeros((10, 64, LANES), F32)
-    for m in range(ORDERS):
-        DACC[m, pl.ds(FIELDS, 56), :] = jnp.zeros((56, LANES), F32)
+    VW[...] = jnp.zeros((ROWS * 8, LANES), F32)
+    UV[...] = jnp.zeros((ROWS * 16, LANES), F32)
 
     for copy in halo:
         copy.wait_recv()
@@ -217,90 +229,107 @@
     sub_k = iota((K, LANES), 0)
 
     def order_zero(base, n, part, first):
-        def body(i, carry):
-            rho = base + i
-            g = my_row * ROWS + rho - GHOST
-            row_mask = ((g >= 0) & (g < grid_rows)).astype(F32)
-            at = 4 * (first + i)
-            right = pltpu.roll(RRB[part, :, :], lax.rem(LANES - at, LANES), 1)
-            left = pltpu.roll(RLB[part, :, :], lax.rem(2 * LANES - 4 - at, LANES), 1)
-            ms = side_mask * row_mask
-            side = jnp.where(lane_k < 4, right, left) * ms
-            mid = X[0, rho, :, :] * row_mask
-            mc = jnp.ones((1, LANES), F32) * row_mask
-            for half, (v, m) in enumerate(((mid, mc), (side, ms))):
-                d = v[R : R + 1, :]
-                s = v[R + 1 : R + 2, :]
-                CF[5 * half, pl.ds(rho + 4, 1), :] = 2.0 * d * m
-                CF[5 * half + 1, pl.ds(rho + 4, 1), :] = (2.0 * COUPLING) * m
-                CF[5 * half + 2, pl.ds(rho + 4, 1), :] = 2.0 * (s - COUPLING) * m
-                CF[5 * half + 3, pl.ds(rho + 4, 1), :] = 2.0 * (s + COUPLING) * m
-                CF[5 * half + 4, pl.ds(rho + 4, 1), :] = m
-            X[0, rho, :, :] = jnp.where(sub_k < R, mid, 0.0)
-            SD[0, rho, :, :] = jnp.where(sub_k < R, side, 0.0)
+        def body(b, carry):
+            stores = []
+            for k in range(4):
+                i = 4 * b + k
+                rho = base + i
+                g = my_row * ROWS + rho - GHOST
+                row_mask = ((g >= 0) & (g < grid_rows)).astype(F32)
+                at = 4 * (first + i)
+                right = pltpu.roll(RRB[part, :, :], lax.rem(LANES - at, LANES), 1)
+                left = pltpu.roll(RLB[part, :, :], lax.rem(2 * LANES - 4 - at, LANES), 1)
+                ms = side_mask * row_mask
+                side = jnp.where(lane_k < 4, right, left) * ms
+                mid = X[0][line(rho), :] * row_mask
+                mc = jnp.ones((1, LANES), F32) * row_mask
+                stores.append((rho, (mid, mc), (side, ms)))
+            for rho, mid, side in stores:
+                for half, (v, m) in enumerate((mid, side)):
+                    d = v[R : R + 1, :]
+                    s = v[R + 1 : R + 2, :]
+                    CF[5 * half, pl.ds(rho + 4, 1), :] = 2.0 * d * m
+                    CF[5 * half + 1, pl.ds(rho + 4, 1), :] = (2.0 * COUPLING) * m
+                    CF[5 * half + 2, pl.ds(rho + 4, 1), :] = 2.0 * (s - COUPLING) * m
+                    CF[5 * half + 3, pl.ds(rho + 4, 1), :] = 2.0 * (s + COUPLING) * m
+                    CF[5 * half + 4, pl.ds(rho + 4, 1), :] = m
+                X[0][line(rho), :] = jnp.where(sub_k < R, mid[0], 0.0)
+                SD[0][line(rho), :] = jnp.where(sub_k < R, side[0], 0.0)
             return carry
 
-        lax.fori_loop(0, n, body, 0)
+        lax.fori_loop(0, n // 4, body, 0)
 
     order_zero(0, 4, 0, 12)
     order_zero(4, 32, 1, 0)
     order_zero(36, 16, 2, 0)
     order_zero(52, 4, 3, 0)
 
-    def copy_zero(r, carry):
-        T[pl.ds(pl.multiple_of(r * FIELDS, 8), K), :] = X[0, r + GHOST, :, :]
+    def images(m, n):
+        def body(b, carry):
+            mids, sides = [], []
+            for k in range(n):
+                rho = m + n * b + k
+                c = X[m - 1][line(rho), :]
+                s = SD[m - 1][line(rho), :]
+                cu = X[m - 1][line(rho - 1), :] + X[m - 1][line(rho + 1), :]
+                cl, sl = pltpu.roll(c, 1, 1), pltpu.roll(s, 1, 1)
+                cr, sr = pltpu.roll(c, 127, 1), pltpu.roll(s, 127, 1)
+
+                def row(kind):
+                    return CF[kind, pl.ds(rho + 4, 1), :]
+
+                left = jnp.where(lane_k == 0, sl, cl)
+                right = jnp.where(lane_k == 127, sr, cr)
+                new = row(0) * c - row(1) * cu + row(2) * right - row(3) * left
+                mids.append(0.5 * new if m == 1 else new - X[m - 2][line(rho), :])
+                if m < 4:
+                    su = SD[m - 1][line(rho - 1), :] + SD[m - 1][line(rho + 1), :]
+                    left = jnp.where(lane_k == 0, cl, sl)
+                    right = jnp.where(lane_k == 127, cr, sr)
+                    side = row(5) * s - row(6) * su + row(7) * right - row(8) * left
+                    sides.append(0.5 * side if m == 1 else side - SD[m - 2][line(rho), :])
+            for k in range(n):
+                rho = m + n * b + k
+                X[m][line(rho), :] = mids[k]
+                if m < 4:
+                    SD[m][line(rho), :] = sides[k]
+            return carry
+
+        lax.fori_loop(0, (ROWS + 8 - 2 * m) // n, body, 0)
+
+    for m, n in zip(range(1, ORDERS), (6, 4, 5, 6)):
+        images(m, n)
+
+    ACC[...] = jnp.zeros((256 + PADDED, 256), F32)
+    AHL[pl.ds(PADDED, 256 - PADDED), :] = jnp.zeros((256 - PADDED, ROWS * LANES), jnp.bfloat16)
+
+    def lines(first, n):
+        blank = [jnp.zeros((PADDED - FIELDS, LANES), F32)]
+        return jnp.concatenate(
+            [
+                jnp.concatenate([X[m][line(first + k + GHOST), :] for m in range(ORDERS)] + blank, axis=0)
+                for k in range(n)
+            ],
+            axis=1,
+        )
+
+    def bdot(a, b):
+        return lax.dot_general(a, b, (((1,), (1,)), ((), ())), preferred_element_type=F32)
+
+    def gram_rows(g, carry):
+        for part in range(4):
+            a = lines(GROUP * g + 2 * part, 2)
+            hi = a.astype(jnp.bfloat16)
+            at = pl.ds(pl.multiple_of((GROUP * g + 2 * part) * LANES, LANES), 2 * LANES)
+            AHL[pl.ds(0, PADDED), at] = hi
+            AHL[pl.ds(256, PADDED), at] = (a - hi.astype(F32)).astype(jnp.bfloat16)
+        at = pl.ds(pl.multiple_of(GROUP * g * LANES, LANES), GROUP * LANES)
+        ACC[:, pl.ds(0, PADDED)] += bdot(AHL[:, at], AHL[pl.ds(0, PADDED), at])
         return carry
 
-    lax.fori_loop(0, ROWS, copy_zero, 0)
-
-    def images(m):
-        def body(i, carry):
-            rho = m + i
-            c = X[m - 1, rho, :, :]
-            s = SD[m - 1, rho, :, :]
-            cu = X[m - 1, rho - 1, :, :] + X[m - 1, rho + 1, :, :]
-            cl, sl = pltpu.roll(c, 1, 1), pltpu.roll(s, 1, 1)
-            cr, sr = pltpu.roll(c, 127, 1), pltpu.roll(s, 127, 1)
-
-            def row(kind):
-                return CF[kind, pl.ds(rho + 4, 1), :]
-
-            left = jnp.where(lane_k == 0, sl, cl)
-            right = jnp.where(lane_k == 127, sr, cr)
-            new = row(0) * c - row(1) * cu + row(2) * right - row(3) * left
-            new = 0.5 * new if m == 1 else new - X[m - 2, rho, :, :]
-            if m < 4:
-                X[m, rho, :, :] = new
-                su = SD[m - 1, rho - 1, :, :] + SD[m - 1, rho + 1, :, :]
-                left = jnp.where(lane_k == 0, cl, sl)
-                right = jnp.where(lane_k == 127, cr, sr)
-                side = row(5) * s - row(6) * su + row(7) * right - row(8) * left
-                SD[m, rho, :, :] = 0.5 * side if m == 1 else side - SD[m - 2, rho, :, :]
-
-                @pl.when((rho >= GHOST) & (rho < GHOST + ROWS))
-                def _():
-                    at = pl.multiple_of((rho - GHOST) * FIELDS + m * K, 8)
-                    T[pl.ds(at, K), :] = new
-            else:
-                at = pl.multiple_of((rho - GHOST) * FIELDS + m * K, 8)
-                T[pl.ds(at, K), :] = new
-            return carry
-
-        lax.fori_loop(0, ROWS + 8 - 2 * m, body, 0)
-
-    for m in range(1, ORDERS):
-        images(m)
-
-    ACC[...] = jnp.zeros((FIELDS, 256), F32)
-
-    def gram_rows(g, carry):
-        a = jnp.concatenate(
-            [T[pl.ds(pl.multiple_of((4 * g + k) * FIELDS, 8), FIELDS), :] for k in range(4)], axis=1
-        )
-        ACC[:, pl.ds(0, FIELDS)] += dot(a, a, 1, 1)
-        return carry
-
-    lax.fori_loop(0, ROWS // 4, gram_rows, 0)
+    lax.fori_loop(0, ROWS // GROUP, gram_rows, 0)
+    cross = jnp.concatenate([ACC[pl.ds(256, PADDED), :], jnp.zeros((256 - PADDED, 256), F32)], axis=0)
+    ACC[pl.ds(0, PADDED), :] = ACC[pl.ds(0, PADDED), :] + cross[0:PADDED, :] + jnp.transpose(cross)[0:PADDED, :]
 
     def strip(ref, a, shift):
         v = ref[pl.ds(a * K, K), :]
@@ -400,13 +429,20 @@
         h = 2.0 * h1 - dot(h1, GB0[pl.ds(0, LANES), :], 1, 0)
         h_wide = jnp.concatenate([h, jnp.zeros((8, LANES), F32)], axis=1)
         raw = dot(cw - h_wide, LB[...], 1, 0)
-        raw_col = jnp.transpose(raw)[0:FIELDS, 0:1]
-        CB[...] = jnp.broadcast_to(raw_col, (FIELDS, LANES))
+        raw_col = jnp.transpose(raw)[0 : FIELDS + 16, 0:1]
+        CB[...] = jnp.broadcast_to(raw_col, (FIELDS + 16, LANES))
 
         def combine(i, carry):
             for k in range(8):
-                at = pl.multiple_of((8 * i + k) * FIELDS, 8)
-                value = jnp.sum(CB[...] * T[pl.ds(at, FIELDS), :], axis=0, keepdims=True)
+                rho = 8 * i + k + GHOST
+                value = CB[pl.ds(0, K), :] * X[0][line(rho), :]
+                for m in range(1, ORDERS):
+                    value = value + CB[pl.ds(m * K, K), :] * X[m][line(rho), :]
+                value = jnp.sum(value, axis=0, keepdims=True)
+                if s:
+                    at = pl.multiple_of(16 * (8 * i + k), 8)
+                    older = CB[pl.ds(FIELDS, 16), :] * UV[pl.ds(at, 16), :]
+                    value = value + jnp.sum(older, axis=0, keepdims=True)
                 U0[s, pl.ds(8 * i + k, 1), :] = value
             return carry
 
@@ -479,23 +515,24 @@
             orders.append(now[0])
         for m in range(ORDERS):
             VB[m, :, :] = orders[m][8:56, :]
-            T[pl.ds(m * K + r, ROWS, stride=FIELDS), :] = orders[m][8:56, :]
-
-        for a in range(ORDERS):
-            def products(i, accs):
-                at = pl.multiple_of(i * FIELDS + a * K, 8)
-                t = T[pl.ds(at, K), :]
-                return tuple(acc + t * VB[m, pl.ds(i, 1), :] for m, acc in enumerate(accs))
-
-            accs = lax.fori_loop(
-                0, ROWS, products, tuple(jnp.zeros((K, LANES), F32) for _ in range(ORDERS))
-            )
-            for m in range(ORDERS):
-                DACC[m, pl.ds(a * K, K), :] = accs[m]
-        d = jnp.zeros((8, 256), F32)
-        for m in range(ORDERS):
-            pick = (iota((8, LANES), 0) == m).astype(F32)
-            d = d + dot(pick, DACC[m], 1, 1)
+            VW[pl.ds(m, ROWS, stride=8), :] = orders[m][8:56, :]
+            UV[pl.ds(5 * s + m, ROWS, stride=16), :] = orders[m][8:56, :]
+
+        v = jnp.concatenate([VW[pl.ds(8 * k, 8), :] for k in range(ROWS)], axis=1)
+        w = jnp.concatenate([UV[pl.ds(16 * k, 16), :] for k in range(ROWS)], axis=1)
+        v_hi = v.astype(jnp.bfloat16).astype(F32)
+        w_hi = w.astype(jnp.bfloat16).astype(F32)
+        v = jnp.concatenate([v_hi, v - v_hi], axis=0).astype(jnp.bfloat16)
+        w = jnp.concatenate([w_hi, w - w_hi], axis=0).astype(jnp.bfloat16)
+        old = bdot(v, AHL[...])
+        new = bdot(v, w)
+        new = new[0:8, :] + new[8:16, :]
+        DN[...] = jnp.zeros((8, 256), F32)
+        DN[:, pl.ds(FIELDS, 16)] = new[:, 0:16] + new[:, 16:32]
+        old = old[0:8, :] + old[8:16, :]
+        d = old[:, 0:256] + jnp.concatenate([old[:, 256:], jnp.zeros((8, 256 - PADDED), F32)], axis=1)
+        d = jnp.where(lane8 < FIELDS, d, 0.0)
+        d = d + DN[...]
 
         total = d
         sem = 0
@@ -516,7 +553,7 @@
                 total = total + box[i]
         d = total * inverse_total
 
-        nn = jnp.sum(jnp.where(lane_r == r, d[0:1, :], 0.0), axis=1, keepdims=True)
+        nn = jnp.sum(jnp.where(lane_r == FIELDS + 5 * s, d[0:1, :], 0.0), axis=1, keepdims=True)
         beta = jnp.sqrt(nn + EPSILON)
         ib = 1.0 / beta
         eta = jnp.sqrt(e2_square + beta * beta + EPSILON)
@@ -529,8 +566,8 @@
         newi_ref[s, :, :] = VB[4] * ib
         for m in range(ORDERS):
             at = m * K + r
-            LB[pl.ds(at, 1), :] = jnp.where(lane_r == at, ib, 0.0)
-            GS[pl.ds(at, 1), :] = d[m : m + 1, :]
+            LB[pl.ds(at, 1), :] = jnp.where(lane_r == FIELDS + 5 * s + m, ib, 0.0)
+            GS[pl.ds(FIELDS + 5 * s + m, 1), :] = d[m : m + 1, :]
         if s + 1 < STEPS:
             db = dot(d, LB[...], 1, 1) * ib
             dcol = jnp.transpose(db)[:, 0:1]
@@ -540,15 +577,12 @@
                 GB0[pl.ds(m * K + r, 1), :] = jnp.where(lane1 < K, db[m : m + 1, 0:LANES], 0.0)
 
     mirrored = jnp.transpose(GS[...])
-    field = lane_w
-    for a in range(1, ORDERS):
-        field = field - jnp.where(lane_w >= a * K, K, 0)
-    age_col = jnp.maximum(field - (R - 1), 0)
-    age_row = jnp.maximum(iota((K, 256), 0) - (R - 1), 0)
-    for a in range(ORDERS):
-        GS[pl.ds(a * K, K), :] = jnp.where(
-            age_row >= age_col, GS[pl.ds(a * K, K), :], mirrored[a * K : (a + 1) * K, :]
-        )
+    def age(index):
+        return sum(((index >= FIELDS + 5 * t).astype(jnp.int32) for t in range(1, STEPS)), (index >= FIELDS).astype(jnp.int32))
+
+    whole_row = age(iota((256, 256), 0))
+    whole_col = age(iota((256, 256), 1))
+    GS[...] = jnp.where(whole_row >= whole_col, GS[...], mirrored)
     gram = dot(dot(LB[...], GS[...], 1, 0), LB[...], 1, 1)
     gram_ref[...] = gram[0:FIELDS, 0:FIELDS]
     mcol = jnp.transpose(MT[...])
@@ -573,15 +607,17 @@
     big_copies = sum(n - 1 for n in counts) + counts[0] - 1
     small_copies = sum(n - 1 for n in counts)
     vmem = lambda *shape: pltpu.VMEM(shape, F32)
+    half = lambda *shape: pltpu.VMEM(shape, jnp.bfloat16)
     dma = lambda *shape: pltpu.SemaphoreType.DMA(shape)
     scratch = [
-        vmem(4, ROWS + 8, K, LANES), vmem(4, ROWS + 8, K, LANES), vmem(ROWS * FIELDS, LANES),
+        [vmem((ROWS + 8) * K, LANES) for _ in range(ORDERS)],
+        [vmem((ROWS + 8) * K, LANES) for _ in range(ORDERS - 1)],
         vmem(10, 64, LANES), vmem(2, K, LANES), vmem(2, K, LANES), vmem(4, K, LANES), vmem(4, K, LANES),
-        vmem(FIELDS, 256), vmem(256, LANES), vmem(256, LANES), vmem(256, 256), vmem(256, 256),
-        vmem(256, LANES), vmem(FIELDS, LANES), vmem(LANES, 256), vmem(LANES, LANES), vmem(256, LANES),
+        half(256 + PADDED, ROWS * LANES), vmem(256 + PADDED, 256), vmem(256, LANES), vmem(256, LANES), vmem(256, 256), vmem(256, 256),
+        vmem(256, LANES), vmem(FIELDS + 16, LANES), vmem(LANES, 256), vmem(LANES, LANES), vmem(256, LANES),
         vmem(STEPS, ROWS, LANES), vmem(STEPS, 8, LANES), vmem(STEPS, 8, LANES), vmem(STEPS, 8, LANES),
         vmem(STEPS, 3, 8, LANES), vmem(STEPS, 3, 8, LANES), vmem(ORDERS, ROWS, LANES),
-        vmem(ORDERS, 256, LANES),
+        vmem(ROWS * 8, LANES), vmem(ROWS * 16, LANES), vmem(8, 256),
         [vmem(n, chunk, LANES) for n in counts],
         [vmem(STEPS, n, 8, 256) for n in counts],
         dma(8), dma(8), dma(big_copies), dma(big_copies),

time: 145 us -> 115 us (0.79)
  Pallas kernels: 138 us -> 109 us
    pallas_call x1, Pallas kernels: 138 us -> 109 us  [local(): pl.pallas_call(functools.partial(kernel, sizes), out_shape=[shape(STEPS,...]
where the time goes in v1:
time: 115 us
  Pallas kernels  109 us (95%)
  local copies, waits for them, and re-layouts  5.84 us (5%)
    pallas_call x1, Pallas kernels, local(): pl.pallas_call(functools.partial(kernel, sizes), out_shape=[shape(STEPS,...  109 us
    unnamed x12, local copies, waits for them, and re-layouts  5.64 us

profile of v1, /device:TPU:2, one launch (start us, length us, event | category | flops | bytes accessed | tf_op | source)
XLA Modules:
  0.0 115.0 jit_solution(10446041163931312390)
XLA Ops:
  0.6 0.0 copy-start.1
  0.6 0.0 copy-start.2
  0.7 1.0 copy.12.kr_ref
  1.7 0.0 copy-done.1
  1.7 0.0 copy-done.2
  1.7 0.0 copy-start
  1.7 1.2 %copy-done = f32[37,48,128]{2,1,0:T(8,128)S(1)} copy-done((f32[37,48,128]{2,1,0:T(8,128)S(1)}, f32[37,48,128]{2,1,0:T(8,128)}, u32[]{:S(2)}) %copy-start) | copy-done | bytes 909336
  2.8 108.5 %shard_map.83 = (f32[3,48,128]{2,1,0:T(8,128)S(1)}, f32[4,40,37]{2,1,0:T(8,128)S(1)}, f32[3,37]{1,0:T(4,128)S(1)}, f32[200,200]{1,0:T(8,128)S(1)}, f32[3,48,128]{2,1,0:T(8,128)S(1)}) custom-call(f32[1776,128]{1,0:T(8,128)S(1)} %bitcast.1, f32[4,37,34]{2,1,0:T(8,128)S(1)} %copy.12.kr_ref, f32[48,128]{1,0:T(8,128)S(1)} %copy-done.1, f32[48,128]{1,0:T(8,128)S(1)} %copy-done.2), custom_call_target="tpu_custom_call" | custom-call | tf_op jit(solution)/shard_map/pallas_call | solution.py:627
  111.4 0.7 copy.13
  112.1 0.2 reshape.17
  112.3 0.9 copy.14
  113.2 0.6 copy.18
  113.8 0.6 copy.19
  114.4 0.6 copy.20
Async XLA Ops:
  0.6 1.0 copy-start.1
  0.6 1.0 copy-start.2
  1.7 1.2 %copy-start = (f32[37,48,128]{2,1,0:T(8,128)S(1)}, f32[37,48,128]{2,1,0:T(8,128)}, u32[]{:S(2)}) copy-start(f32[37,48,128]{2,1,0:T(8,128)} %param.4) | copy-start | bytes 2727940

commit v2 on v1

--- a/solution.py
+++ b/solution.py
@@ -28,12 +28,20 @@
 GHOST = 4
 PADDED = 208
 GROUP = 8
+FIRST = 128
+SECOND = 192
 F32 = jnp.float32
 
 
 def dot(a, b, ca, cb):
     return lax.dot_general(
         a, b, (((ca,), (cb,)), ((), ())), precision=HIGHEST, preferred_element_type=F32
+    )
+
+
+def dot3(a, b, ca, cb):
+    return lax.dot_general(
+        a, b, (((ca,), (cb,)), ((), ())), precision=lax.Precision.HIGH, preferred_element_type=F32
     )
 
 
@@ -112,12 +120,13 @@
 
 
 def kernel(
-    sizes, x_ref, kr_ref, st_ref, ro_ref,
+    sizes, x_hbm, kr_hbm, st_hbm, ro_hbm,
     newc_ref, coef_ref, hess_ref, gram_ref, newi_ref,
-    X, SD, CF, PL, PR, RRB, RLB, AHL, ACC, BIG, FULL, GS, LB, GB0, CB, MT, HS, KS,
+    x_ref, kr_ref, st_ref, ro_ref, in_sem,
+    X, SD, CF, PL, PR, RRB, RLB, AHL, ACC, AC0, BIG, FULL, BIG2, FULL2, GS, GC, LB, GB0, CB, MT, HS, KS,
     U0, PK, HT, HB, KRB, KLB, VB, VW, UV, DN,
-    slots_big, slots_small,
-    hsend, hrecv, bsend, brecv, usend, urecv, ssend, srecv,
+    slots_big, slots_two, slots_small, slots_last, slots_late,
+    hsend, hrecv, bsend, brecv, csend, crecv, usend, urecv, ssend, srecv, lsend, lrecv,
 ):
     nrow = sizes["x"] * sizes["core"]
     ncol = sizes["y"] * sizes["z"]
@@ -127,6 +136,15 @@
     inverse_total = 1.0 / (grid_rows * ncol * LANES)
     stage_offsets = [offsets(sizes, axes) for axes in STAGES]
     pending = []
+
+    loads = [
+        pltpu.make_async_copy(src, dst, in_sem.at[i])
+        for i, (src, dst) in enumerate(
+            ((x_hbm, x_ref), (st_hbm, st_ref), (ro_hbm, ro_ref), (kr_hbm, kr_ref))
+        )
+    ]
+    for copy in loads:
+        copy.start()
 
     barrier = pltpu.get_barrier_semaphore()
     count = 0
@@ -163,6 +181,8 @@
             X[0][pl.ds(at + R + 2, 1), :] = jnp.zeros((1, LANES), F32)
         return carry
 
+    for copy in loads[:3]:
+        copy.wait()
     lax.fori_loop(0, ROWS // 4, load_rows, 0)
     lane_k = iota((K, LANES), 1)
 
@@ -200,21 +220,24 @@
         send(PR.at[1], RLB.at[0], hsend.at[7], hrecv.at[7], near(sizes, 1, 1)),
     ]
 
-    KS[...] = jnp.zeros((256, LANES), F32)
+    loads[3].wait()
+    KS[...] = jnp.zeros((K, 256), F32)
     for j in range(4):
-        KS[pl.ds(j * K, R), pl.ds(0, KRYLOV)] = kr_ref[j]
-    pt = jnp.transpose(KS[...])[0:K, :]
-    kgram = dot(pt, KS[...], 1, 0)
+        KS[pl.ds(0, KRYLOV), pl.ds(j * K, R)] = kr_ref[:, j, :]
+    pt = KS[...]
+    kgram = dot(pt, pt, 1, 1)
+    kgram = jnp.concatenate([kgram, jnp.zeros((K, LANES - K), F32)], axis=1)
     kinv = forward_inverse(augmented(kgram, 0.0, KRYLOV), KRYLOV)
     MT[...] = jnp.zeros((LANES, 256), F32)
     MT[pl.ds(0, K), :] = dot(kinv[:, 0:K], pt, 1, 0)
     HS[...] = jnp.zeros((LANES, LANES), F32)
     LB[...] = jnp.zeros((256, 256), F32)
     GS[...] = jnp.zeros((256, 256), F32)
-    BIG[...] = jnp.zeros((256, LANES), F32)
+    BIG[...] = jnp.zeros((FIRST, LANES), F32)
+    BIG2[...] = jnp.zeros((SECOND, LANES), F32)
     CF[...] = jnp.zeros((10, 64, LANES), F32)
     VW[...] = jnp.zeros((ROWS * 8, LANES), F32)
-    UV[...] = jnp.zeros((ROWS * 16, LANES), F32)
+    UV[...] = jnp.zeros((ROWS * 24, LANES), F32)
 
     for copy in halo:
         copy.wait_recv()
@@ -300,7 +323,7 @@
     for m, n in zip(range(1, ORDERS), (6, 4, 5, 6)):
         images(m, n)
 
-    ACC[...] = jnp.zeros((256 + PADDED, 256), F32)
+    AC0[...] = jnp.zeros((96, 512), F32)
     AHL[pl.ds(PADDED, 256 - PADDED), :] = jnp.zeros((256 - PADDED, ROWS * LANES), jnp.bfloat16)
 
     def lines(first, n):
@@ -316,89 +339,156 @@
     def bdot(a, b):
         return lax.dot_general(a, b, (((1,), (1,)), ((), ())), preferred_element_type=F32)
 
-    def gram_rows(g, carry):
-        for part in range(4):
+    def split_rows(g):
+        for part in range(GROUP // 2):
             a = lines(GROUP * g + 2 * part, 2)
             hi = a.astype(jnp.bfloat16)
             at = pl.ds(pl.multiple_of((GROUP * g + 2 * part) * LANES, LANES), 2 * LANES)
             AHL[pl.ds(0, PADDED), at] = hi
             AHL[pl.ds(256, PADDED), at] = (a - hi.astype(F32)).astype(jnp.bfloat16)
+
+    def gram_rows(g):
+        at = pl.ds(pl.multiple_of(GROUP * g * LANES, LANES), GROUP * LANES)
+        first = jnp.concatenate([AHL[pl.ds(0, 48), at], AHL[pl.ds(256, 48), at]], axis=0)
+        return bdot(first, AHL[:, at])
+
+    def gram_step(g, carry):
+        part = gram_rows(g - 1)
+        split_rows(g)
+        AC0[:, pl.ds(0, 256 + PADDED)] += part
+        return carry
+
+    split_rows(0)
+    lax.fori_loop(1, ROWS // GROUP, gram_step, 0)
+    AC0[:, pl.ds(0, 256 + PADDED)] += gram_rows(ROWS // GROUP - 1)
+    top = AC0[pl.ds(0, K), pl.ds(0, 256)] + AC0[pl.ds(48, K), pl.ds(0, 256)] + AC0[pl.ds(0, K), pl.ds(256, 256)]
+    lane_w = iota((K, 256), 1)
+    top = jnp.where(lane_w < FIELDS, top, 0.0)
+    BIG[pl.ds(0, K), :] = top[:, 0:LANES]
+    BIG[pl.ds(K, K), :] = top[:, LANES:]
+
+    class Reduction:
+        def __init__(self, big, whole, boxes, total_rows, send_sems, recv_sems):
+            self.big, self.whole, self.boxes = big, whole, boxes
+            self.chunk = total_rows // nrow
+            self.send_sems, self.recv_sems, self.sem = send_sems, recv_sems, 0
+            self.own = pl.ds(pl.multiple_of(my_row * self.chunk, 8), self.chunk)
+            self.copies = []
+
+        def emit(self, src, dst, to):
+            self.copies.append(send(src, dst, self.send_sems.at[self.sem], self.recv_sems.at[self.sem], to))
+            self.sem += 1
+
+        def arrived(self):
+            for copy in self.copies:
+                copy.wait_recv()
+            self.copies = []
+
+        def start(self, stage):
+            me = place(sizes, STAGES[stage])
+            box = self.boxes[stage]
+            if stage == 0:
+                box[me] = self.big[self.own, :]
+            for off in stage_offsets[stage]:
+                to = peer_of(sizes, STAGES[stage], off)
+                if stage == 0:
+                    at = pl.multiple_of(linear(sizes, ROW, to) * self.chunk, 8)
+                    self.emit(self.big.at[pl.ds(at, self.chunk)], box.at[me], to)
+                else:
+                    self.emit(box.at[me], box.at[me], to)
+
+        def finish(self, stage):
+            self.arrived()
+            box = self.boxes[stage]
+            total = box[0]
+            for i in range(1, len(stage_offsets[stage]) + 1):
+                total = total + box[i]
+            if stage + 1 < len(STAGES):
+                self.boxes[stage + 1][place(sizes, STAGES[stage + 1])] = total
+            else:
+                self.whole[self.own, :] = total * inverse_total
+
+        def gather(self):
+            for off in stage_offsets[0]:
+                self.emit(self.whole.at[self.own], self.whole.at[self.own], peer_of(sizes, ROW, off))
+
+    class Sum:
+        def __init__(self, boxes, send_sems, recv_sems):
+            self.boxes, self.send_sems, self.recv_sems, self.sem = boxes, send_sems, recv_sems, 0
+
+        def start(self, stage, value):
+            me = place(sizes, STAGES[stage])
+            box = self.boxes[stage]
+            box[me] = value
+            self.copies = []
+            for off in stage_offsets[stage]:
+                to = peer_of(sizes, STAGES[stage], off)
+                sems = self.send_sems.at[self.sem], self.recv_sems.at[self.sem]
+                self.copies.append(send(box.at[me], box.at[me], *sems, to))
+                self.sem += 1
+
+        def finish(self, stage):
+            for copy in self.copies:
+                copy.wait_recv()
+            box = self.boxes[stage]
+            total = box[0]
+            for i in range(1, len(stage_offsets[stage]) + 1):
+                total = total + box[i]
+            return total
+
+    one = Reduction(BIG, FULL, slots_big, FIRST, bsend, brecv)
+    two = Reduction(BIG2, FULL2, slots_two, SECOND, csend, crecv)
+    one.start(0)
+
+    ACC[...] = jnp.zeros((256 + PADDED, 256), F32)
+
+    def gram_rest(g, carry):
         at = pl.ds(pl.multiple_of(GROUP * g * LANES, LANES), GROUP * LANES)
         ACC[:, pl.ds(0, PADDED)] += bdot(AHL[:, at], AHL[pl.ds(0, PADDED), at])
         return carry
 
-    lax.fori_loop(0, ROWS // GROUP, gram_rows, 0)
+    lax.fori_loop(0, ROWS // GROUP, gram_rest, 0)
     cross = jnp.concatenate([ACC[pl.ds(256, PADDED), :], jnp.zeros((256 - PADDED, 256), F32)], axis=0)
     ACC[pl.ds(0, PADDED), :] = ACC[pl.ds(0, PADDED), :] + cross[0:PADDED, :] + jnp.transpose(cross)[0:PADDED, :]
 
-    def strip(ref, a, shift):
-        v = ref[pl.ds(a * K, K), :]
-        return pltpu.roll(v, shift % 256, 1) if shift % 256 else v
+    def strip(a, shift):
+        return pltpu.roll(ACC[pl.ds(a * K, K), :], shift % 256, 1)[:, 0:LANES]
 
     lane_n = iota((K, LANES), 1)
-    last = lane_n >= 80
-    BIG[pl.ds(0, K), :] = strip(ACC, 0, 0)[:, 0:LANES]
-    BIG[pl.ds(K, K), :] = strip(ACC, 1, -40)[:, 0:LANES]
-    BIG[pl.ds(2 * K, K), :] = strip(ACC, 2, -80)[:, 0:LANES]
-    BIG[pl.ds(3 * K, K), :] = jnp.where(last, strip(ACC, 4, -80)[:, 0:LANES], strip(ACC, 0, -120)[:, 0:LANES])
-    BIG[pl.ds(4 * K, K), :] = jnp.where(last, strip(ACC, 1, -80)[:, 0:LANES], strip(ACC, 3, -120)[:, 0:LANES])
-
-    chunk = 256 // nrow
-    own = pl.ds(pl.multiple_of(my_row * chunk, 8), chunk)
-
-    def chunk_of(coords):
-        return pl.ds(pl.multiple_of(linear(sizes, ROW, coords) * chunk, 8), chunk)
-
-    sem = 0
-    for stage, (axes, offs) in enumerate(zip(STAGES, stage_offsets)):
-        me = place(sizes, axes)
-        box = slots_big[stage]
-        if stage == 0:
-            box[me] = BIG[own, :]
-        copies = []
-        for off in offs:
-            to = peer_of(sizes, axes, off)
-            src = BIG.at[chunk_of(to)] if stage == 0 else box.at[me]
-            copies.append(send(src, box.at[me], bsend.at[sem], brecv.at[sem], to))
-            sem += 1
-        for copy in copies:
-            copy.wait_recv()
-        total = box[0]
-        for i in range(1, len(offs) + 1):
-            total = total + box[i]
-        if stage + 1 < len(STAGES):
-            slots_big[stage + 1][place(sizes, STAGES[stage + 1])] = total
-        else:
-            FULL[own, :] = total * inverse_total
-    copies = []
-    for off in stage_offsets[0]:
-        to = peer_of(sizes, ROW, off)
-        copies.append(send(FULL.at[own], FULL.at[own], bsend.at[sem], brecv.at[sem], to))
-        sem += 1
-    for copy in copies:
-        copy.wait_recv()
-
-    lane_w = iota((K, 256), 1)
-
-    def wide(a):
-        v = FULL[pl.ds(a * K, K), :]
-        return jnp.concatenate([jnp.where(lane_n < 120, v, 0.0), jnp.zeros((K, LANES), F32)], axis=1)
-
-    g3, g4 = wide(3), wide(4)
-
-    def between(v, lo, hi):
-        return jnp.where((lane_w >= lo) & (lane_w < hi), v, 0.0)
-
-    GS[pl.ds(0, K), :] = wide(0) + between(pltpu.roll(g3, 120, 1), 120, 200)
-    GS[pl.ds(K, K), :] = pltpu.roll(wide(1), 40, 1) + between(pltpu.roll(g4, 80, 1), 160, 200)
-    GS[pl.ds(2 * K, K), :] = pltpu.roll(wide(2), 80, 1)
-    GS[pl.ds(3 * K, K), :] = between(pltpu.roll(g4, 120, 1), 120, 200)
-    GS[pl.ds(4 * K, K), :] = between(pltpu.roll(g3, 80, 1), 160, 200)
-    mirrored = jnp.transpose(GS[...])
-    for a in range(1, ORDERS):
-        GS[pl.ds(a * K, K), :] = jnp.where(
-            lane_w >= a * K, GS[pl.ds(a * K, K), :], mirrored[a * K : (a + 1) * K, :]
-        )
+    BIG2[pl.ds(0, K), :] = strip(1, -40)
+    BIG2[pl.ds(K, K), :] = strip(2, -80)
+    BIG2[pl.ds(2 * K, K), :] = jnp.where(lane_n >= 80, strip(4, -80), strip(3, -120))
+    BIG2[pl.ds(3 * K, K), :] = strip(1, -160)
+
+    for stage in range(3):
+        one.finish(stage)
+        if stage < 2:
+            one.start(stage + 1)
+    one.gather()
+    one.arrived()
+    two.start(0)
+
+    GS[pl.ds(0, K), pl.ds(0, LANES)] = FULL[pl.ds(0, K), :]
+    GS[pl.ds(0, K), pl.ds(LANES, LANES)] = FULL[pl.ds(K, K), :]
+    GC[...] = jnp.transpose(GS[pl.ds(0, LANES), :])
+
+    def assemble_rest():
+        def wide(a):
+            v = FULL2[pl.ds(a * K, K), :]
+            return jnp.concatenate([v, jnp.zeros((K, LANES), F32)], axis=1)
+
+        def moved(v, shift, lo, hi):
+            return jnp.where((lane_w >= lo) & (lane_w < hi), pltpu.roll(v, shift, 1), 0.0)
+
+        GS[pl.ds(K, K), :] = moved(wide(0), 40, 40, 160) + moved(wide(3), 160, 160, 200)
+        GS[pl.ds(2 * K, K), :] = moved(wide(1), 80, 80, 200)
+        GS[pl.ds(3 * K, K), :] = moved(wide(2), 120, 120, 200)
+        GS[pl.ds(4 * K, K), :] = moved(wide(2), 80, 160, 200)
+        mirrored = jnp.transpose(GS[...])
+        for a in range(1, ORDERS):
+            GS[pl.ds(a * K, K), :] = jnp.where(
+                lane_w >= a * K, GS[pl.ds(a * K, K), :], mirrored[a * K : (a + 1) * K, :]
+            )
 
     finv = forward_inverse(augmented(GS[pl.ds(0, K), pl.ds(0, LANES)], GRAM_SHIFT, R), R)
     finv = jnp.where(sub_k < R, finv, 0.0)
@@ -407,10 +497,39 @@
         LB[pl.ds(a * K, K), :] = pltpu.roll(finv_wide, a * K, 1) if a else finv_wide
     square = (iota((LANES, LANES), 0) < K) & (iota((LANES, LANES), 1) < K)
     small = jnp.where(square, LB[pl.ds(0, LANES), pl.ds(0, LANES)], 0.0)
-    GB0[...] = dot(dot(LB[...], GS[:, pl.ds(0, LANES)], 1, 0), small, 1, 1)
+    GB0[...] = dot3(dot3(LB[...], GC[...], 1, 0), small, 1, 1)
 
     lane_r = iota((1, 256), 1)
     lane8 = iota((8, 256), 1)
+    late = [Sum([b.at[s] for b in slots_late], lsend.at[s], lrecv.at[s]) for s in range(STEPS - 1)]
+
+    def paired():
+        v = jnp.concatenate([VW[pl.ds(8 * k, 8), :] for k in range(ROWS)], axis=1)
+        v_hi = v.astype(jnp.bfloat16).astype(F32)
+        return jnp.concatenate([v_hi, v - v_hi], axis=0).astype(jnp.bfloat16)
+
+    def with_old(v):
+        old = bdot(v, AHL[...])
+        old = old[0:8, :] + old[8:16, :]
+        d = old[:, 0:256] + jnp.concatenate([old[:, 256:], jnp.zeros((8, 256 - PADDED), F32)], axis=1)
+        return jnp.where(lane8 < FIELDS, d, 0.0)
+
+    def with_first(v):
+        first = jnp.concatenate([AHL[pl.ds(0, 48), :], AHL[pl.ds(256, 48), :]], axis=0)
+        part = bdot(v, first)
+        return part[0:8, 0:K] + part[8:16, 0:K] + part[0:8, 48 : 48 + K]
+
+    def with_new(v):
+        w = jnp.concatenate([UV[pl.ds(24 * k, 24), :] for k in range(ROWS)], axis=1)
+        w_hi = w.astype(jnp.bfloat16).astype(F32)
+        w = jnp.concatenate([w_hi, w - w_hi], axis=0).astype(jnp.bfloat16)
+        new = bdot(v, w)
+        new = new[0:8, :] + new[8:16, :]
+        return new[:, 0:24] + new[:, 24:48]
+
+    def keep_late(s, total):
+        rows = pl.ds(FIELDS + 8 * s, 8)
+        GS[rows, :] = GS[rows, :] + total * inverse_total
     sub8 = iota((8, 256), 0)
     tile_mask = iota((64, LANES), 1)
 
@@ -425,12 +544,12 @@
         cw = jnp.where(lane_r < K, 0.5 * moved(-80), -0.5 * moved(40))
         cw = jnp.where(lane_r < FIELDS, cw, 0.0)
         cw = jnp.broadcast_to(cw, (8, 256))
-        h1 = dot(cw, GB0[...], 1, 0)
-        h = 2.0 * h1 - dot(h1, GB0[pl.ds(0, LANES), :], 1, 0)
+        h1 = dot3(cw, GB0[...], 1, 0)
+        h = 2.0 * h1 - dot3(h1, GB0[pl.ds(0, LANES), :], 1, 0)
         h_wide = jnp.concatenate([h, jnp.zeros((8, LANES), F32)], axis=1)
-        raw = dot(cw - h_wide, LB[...], 1, 0)
-        raw_col = jnp.transpose(raw)[0 : FIELDS + 16, 0:1]
-        CB[...] = jnp.broadcast_to(raw_col, (FIELDS + 16, LANES))
+        raw = dot3(cw - h_wide, LB[...], 1, 0)
+        raw_col = jnp.transpose(raw)[0 : FIELDS + 24, 0:1]
+        CB[...] = jnp.broadcast_to(raw_col, (FIELDS + 24, LANES))
 
         def combine(i, carry):
             for k in range(8):
@@ -440,7 +559,7 @@
                     value = value + CB[pl.ds(m * K, K), :] * X[m][line(rho), :]
                 value = jnp.sum(value, axis=0, keepdims=True)
                 if s:
-                    at = pl.multiple_of(16 * (8 * i + k), 8)
+                    at = pl.multiple_of(24 * (8 * i + k), 8)
                     older = CB[pl.ds(FIELDS, 16), :] * UV[pl.ds(at, 16), :]
                     value = value + jnp.sum(older, axis=0, keepdims=True)
                 U0[s, pl.ds(8 * i + k, 1), :] = value
@@ -449,6 +568,7 @@
         lax.fori_loop(0, ROWS // 8, combine, 0)
 
         lane_t = iota((8, LANES), 1)
+        sub_t = iota((8, LANES), 0)
         packed = jnp.zeros((8, LANES), F32)
         for q in range(6):
             tile = U0[s, pl.ds(8 * q, 8), :]
@@ -470,6 +590,9 @@
             send(PK.at[s], KLB.at[s, 0], usend.at[s, 7], urecv.at[s, 7], near(sizes, 1, 1)),
         ]
 
+        if s + 1 < STEPS:
+            VW[pl.ds(0, ROWS, stride=8), :] = U0[s]
+            d_old = with_old(paired())
         h_row = h_wide[0:1, :]
         e = jnp.where(lane_r < K, moved(-40), 0.5 * (moved(40) + moved(-40)))
         e = jnp.where(lane_r < 3 * K, e, pltpu.roll(h_row, 3 * K, 1))
@@ -481,6 +604,16 @@
         e2 = e1 - jnp.sum(mt * g2, axis=0, keepdims=True)
         e2_square = jnp.sum(e2 * e2, axis=1, keepdims=True)
 
+        if s == 0:
+            two.finish(0)
+            two.start(1)
+        if s == 1:
+            two.finish(2)
+            two.gather()
+            late[0].start(1, late[0].finish(0))
+        if s == 2:
+            keep_late(0, late[0].finish(2))
+            late[1].start(1, late[1].finish(0))
         for copy in edge:
             copy.wait_recv()
 
@@ -516,44 +649,50 @@
         for m in range(ORDERS):
             VB[m, :, :] = orders[m][8:56, :]
             VW[pl.ds(m, ROWS, stride=8), :] = orders[m][8:56, :]
-            UV[pl.ds(5 * s + m, ROWS, stride=16), :] = orders[m][8:56, :]
-
-        v = jnp.concatenate([VW[pl.ds(8 * k, 8), :] for k in range(ROWS)], axis=1)
-        w = jnp.concatenate([UV[pl.ds(16 * k, 16), :] for k in range(ROWS)], axis=1)
-        v_hi = v.astype(jnp.bfloat16).astype(F32)
-        w_hi = w.astype(jnp.bfloat16).astype(F32)
-        v = jnp.concatenate([v_hi, v - v_hi], axis=0).astype(jnp.bfloat16)
-        w = jnp.concatenate([w_hi, w - w_hi], axis=0).astype(jnp.bfloat16)
-        old = bdot(v, AHL[...])
-        new = bdot(v, w)
-        new = new[0:8, :] + new[8:16, :]
-        DN[...] = jnp.zeros((8, 256), F32)
-        DN[:, pl.ds(FIELDS, 16)] = new[:, 0:16] + new[:, 16:32]
-        old = old[0:8, :] + old[8:16, :]
-        d = old[:, 0:256] + jnp.concatenate([old[:, 256:], jnp.zeros((8, 256 - PADDED), F32)], axis=1)
-        d = jnp.where(lane8 < FIELDS, d, 0.0)
-        d = d + DN[...]
-
-        total = d
-        sem = 0
-        for stage, (axes, offs) in enumerate(zip(STAGES, stage_offsets)):
-            me = place(sizes, axes)
-            box = slots_small[stage].at[s]
-            box[me] = total
-            copies = []
-            for off in offs:
-                copies.append(
-                    send(box.at[me], box.at[me], ssend.at[s, sem], srecv.at[s, sem], peer_of(sizes, axes, off))
-                )
-                sem += 1
-            for copy in copies:
-                copy.wait_recv()
-            total = box[0]
-            for i in range(1, len(offs) + 1):
-                total = total + box[i]
-        d = total * inverse_total
-
-        nn = jnp.sum(jnp.where(lane_r == FIELDS + 5 * s, d[0:1, :], 0.0), axis=1, keepdims=True)
+            UV[pl.ds(8 * s + m, ROWS, stride=24), :] = orders[m][8:56, :]
+
+        v = paired()
+        if s + 1 < STEPS:
+            total_sum = Sum([b.at[s] for b in slots_small], ssend.at[s], srecv.at[s])
+            DN[...] = jnp.zeros((8, 256), F32)
+            DN[:, pl.ds(0, K)] = with_first(v)
+            DN[:, pl.ds(72, 24)] = with_new(v)
+            low = pltpu.roll(DN[:, pl.ds(0, LANES)], 1, 0)
+            wide_row = d_old[0:1, :]
+            packed_new = jnp.where((lane_t >= 72) & (lane_t < 96), DN[0:1, pl.ds(0, LANES)], wide_row[:, LANES:])
+            value = jnp.where(sub_t == 0, wide_row[:, 0:LANES], jnp.where(sub_t == 1, packed_new, low))
+        else:
+            total_sum = Sum(slots_last, ssend.at[s], srecv.at[s])
+            DN[...] = with_old(v)
+            DN[:, pl.ds(FIELDS, 24)] = with_new(v)
+            value = DN[...]
+        for stage in range(3):
+            total_sum.start(stage, value)
+            if stage == 0 and s + 1 < STEPS:
+                rest = jnp.where((lane8 >= K) & (sub8 >= 1) & (sub8 < ORDERS), with_old(v), 0.0)
+            if s == 0 and stage == 2:
+                two.finish(1)
+                two.start(2)
+                late[0].start(0, rest)
+            if s == 1 and stage == 0:
+                two.arrived()
+                assemble_rest()
+            if s == 1 and stage == 2:
+                late[0].start(2, late[0].finish(1))
+                late[1].start(0, rest)
+            if s == 2 and stage == 2:
+                late[1].start(2, late[1].finish(1))
+            value = total_sum.finish(stage)
+        if s + 1 < STEPS:
+            up = pltpu.roll(value, 7, 0)
+            mid = (lane_t >= 72) & (lane_t < 96)
+            left = jnp.where(sub_t == 0, value, jnp.where(lane_t < K, up, 0.0))
+            right = jnp.where((sub_t == 0) | mid, up, 0.0)
+            value = jnp.concatenate([left, right], axis=1)
+        d = value * inverse_total
+        d = jnp.where(sub8 < ORDERS, d, 0.0)
+
+        nn = jnp.sum(jnp.where(lane_r == FIELDS + 8 * s, d[0:1, :], 0.0), axis=1, keepdims=True)
         beta = jnp.sqrt(nn + EPSILON)
         ib = 1.0 / beta
         eta = jnp.sqrt(e2_square + beta * beta + EPSILON)
@@ -566,32 +705,43 @@
         newi_ref[s, :, :] = VB[4] * ib
         for m in range(ORDERS):
             at = m * K + r
-            LB[pl.ds(at, 1), :] = jnp.where(lane_r == FIELDS + 5 * s + m, ib, 0.0)
-            GS[pl.ds(FIELDS + 5 * s + m, 1), :] = d[m : m + 1, :]
+            LB[pl.ds(at, 1), :] = jnp.where(lane_r == FIELDS + 8 * s + m, ib, 0.0)
+        GS[pl.ds(FIELDS + 8 * s, 8), :] = d
         if s + 1 < STEPS:
-            db = dot(d, LB[...], 1, 1) * ib
+            db = dot3(d, LB[...], 1, 1) * ib
             dcol = jnp.transpose(db)[:, 0:1]
             lane_g = iota((256, LANES), 1)
             GB0[...] = jnp.where(lane_g == r, dcol, GB0[...])
             for m in range(ORDERS):
                 GB0[pl.ds(m * K + r, 1), :] = jnp.where(lane1 < K, db[m : m + 1, 0:LANES], 0.0)
 
+    keep_late(1, late[1].finish(2))
     mirrored = jnp.transpose(GS[...])
     def age(index):
-        return sum(((index >= FIELDS + 5 * t).astype(jnp.int32) for t in range(1, STEPS)), (index >= FIELDS).astype(jnp.int32))
+        return sum(((index >= FIELDS + 8 * t).astype(jnp.int32) for t in range(1, STEPS)), (index >= FIELDS).astype(jnp.int32))
 
     whole_row = age(iota((256, 256), 0))
     whole_col = age(iota((256, 256), 1))
     GS[...] = jnp.where(whole_row >= whole_col, GS[...], mirrored)
-    gram = dot(dot(LB[...], GS[...], 1, 0), LB[...], 1, 1)
-    gram_ref[...] = gram[0:FIELDS, 0:FIELDS]
-    mcol = jnp.transpose(MT[...])
+    gram = dot3(dot3(LB[...], GS[...], 1, 0), LB[...], 1, 1)
+    for a in range(ORDERS):
+        for b in range(ORDERS):
+            gram_ref[a, b, :, :] = gram[a * K : (a + 1) * K, b * K : (b + 1) * K]
     for j in range(4):
-        coef_ref[j, :, :] = mcol[j * K : (j + 1) * K, 0 : KRYLOV + STEPS]
+        coef_ref[:, j, :] = MT[pl.ds(0, KRYLOV + STEPS), pl.ds(j * K, K)]
     hess_ref[...] = jnp.transpose(HS[...])[0:STEPS, 0 : KRYLOV + STEPS]
 
     for copy in pending:
         copy.wait_send()
+
+
+def handed_out(*refs):
+    sources, targets, sems = refs[:5], refs[5:10], refs[10]
+    copies = [pltpu.make_async_copy(a, b, sems.at[i]) for i, (a, b) in enumerate(zip(sources, targets))]
+    for copy in copies:
+        copy.start()
+    for copy in copies:
+        copy.wait()
 
 
 def local(sizes, basis_raw, krylov_raw, stiffness, rotation):
@@ -603,41 +753,62 @@
         for a in axes:
             n *= sizes[a]
         counts.append(n)
-    chunk = 256 // nrow
     big_copies = sum(n - 1 for n in counts) + counts[0] - 1
     small_copies = sum(n - 1 for n in counts)
     vmem = lambda *shape: pltpu.VMEM(shape, F32)
     half = lambda *shape: pltpu.VMEM(shape, jnp.bfloat16)
     dma = lambda *shape: pltpu.SemaphoreType.DMA(shape)
     scratch = [
+        vmem(R * ROWS, LANES), vmem(KRYLOV, 4, R), vmem(ROWS, LANES), vmem(ROWS, LANES), dma(4),
         [vmem((ROWS + 8) * K, LANES) for _ in range(ORDERS)],
         [vmem((ROWS + 8) * K, LANES) for _ in range(ORDERS - 1)],
         vmem(10, 64, LANES), vmem(2, K, LANES), vmem(2, K, LANES), vmem(4, K, LANES), vmem(4, K, LANES),
-        half(256 + PADDED, ROWS * LANES), vmem(256 + PADDED, 256), vmem(256, LANES), vmem(256, LANES), vmem(256, 256), vmem(256, 256),
-        vmem(256, LANES), vmem(FIELDS + 16, LANES), vmem(LANES, 256), vmem(LANES, LANES), vmem(256, LANES),
+        half(256 + PADDED, ROWS * LANES), vmem(256 + PADDED, 256), vmem(96, 512),
+        vmem(FIRST, LANES), vmem(FIRST, LANES), vmem(SECOND, LANES), vmem(SECOND, LANES),
+        vmem(256, 256), vmem(256, LANES), vmem(256, 256),
+        vmem(256, LANES), vmem(FIELDS + 24, LANES), vmem(LANES, 256), vmem(LANES, LANES), vmem(K, 256),
         vmem(STEPS, ROWS, LANES), vmem(STEPS, 8, LANES), vmem(STEPS, 8, LANES), vmem(STEPS, 8, LANES),
         vmem(STEPS, 3, 8, LANES), vmem(STEPS, 3, 8, LANES), vmem(ORDERS, ROWS, LANES),
-        vmem(ROWS * 8, LANES), vmem(ROWS * 16, LANES), vmem(8, 256),
-        [vmem(n, chunk, LANES) for n in counts],
-        [vmem(STEPS, n, 8, 256) for n in counts],
-        dma(8), dma(8), dma(big_copies), dma(big_copies),
+        vmem(ROWS * 8, LANES), vmem(ROWS * 24, LANES), vmem(8, 256),
+        [vmem(n, FIRST // nrow, LANES) for n in counts],
+        [vmem(n, SECOND // nrow, LANES) for n in counts],
+        [vmem(STEPS - 1, n, 8, LANES) for n in counts],
+        [vmem(n, 8, 256) for n in counts],
+        [vmem(STEPS - 1, n, 8, 256) for n in counts],
+        dma(8), dma(8), dma(big_copies), dma(big_copies), dma(big_copies), dma(big_copies),
         dma(STEPS, 8), dma(STEPS, 8), dma(STEPS, small_copies), dma(STEPS, small_copies),
+        dma(STEPS - 1, small_copies), dma(STEPS - 1, small_copies),
     ]
     shape = lambda *dims: jax.ShapeDtypeStruct(dims, F32)
-    new_columns, coefficients, hessenberg, gram, new_images = pl.pallas_call(
+    shapes = [
+        shape(STEPS, ROWS, LANES), shape(width, 4, K), shape(STEPS, width),
+        shape(ORDERS, ORDERS, K, K), shape(STEPS, ROWS, LANES),
+    ]
+    results = pl.pallas_call(
         functools.partial(kernel, sizes),
-        out_shape=[
-            shape(STEPS, ROWS, LANES), shape(4, K, width), shape(STEPS, width),
-            shape(FIELDS, FIELDS), shape(STEPS, ROWS, LANES),
-        ],
-        in_specs=[pl.BlockSpec(memory_space=pltpu.VMEM)] * 4,
+        out_shape=shapes,
+        in_specs=[pl.BlockSpec(memory_space=pltpu.HBM)] * 4,
         out_specs=[pl.BlockSpec(memory_space=pltpu.VMEM)] * 5,
         scratch_shapes=scratch,
         compiler_params=pltpu.CompilerParams(
-            collective_id=0, has_side_effects=True, vmem_limit_bytes=48 * 1024 * 1024
+            collective_id=0, has_side_effects=True, vmem_limit_bytes=55_000_000
         ),
-    )(basis_raw.reshape(R * ROWS, LANES), krylov_raw, stiffness, rotation)
-    return new_columns, coefficients, hessenberg, gram.reshape(ORDERS, K, ORDERS, K), new_images
+    )(
+        basis_raw.reshape(R * ROWS, LANES), jnp.transpose(krylov_raw, (2, 0, 1)),
+        stiffness, rotation,
+    )
+    new_columns, coefficients, hessenberg, gram, new_images = pl.pallas_call(
+        handed_out,
+        out_shape=shapes,
+        in_specs=[pl.BlockSpec(memory_space=pltpu.VMEM)] * 5,
+        out_specs=[pl.BlockSpec(memory_space=pltpu.HBM)] * 5,
+        scratch_shapes=[pltpu.SemaphoreType.DMA((5,))],
+        compiler_params=pltpu.CompilerParams(vmem_limit_bytes=2 * 1024 * 1024),
+    )(*results)
+    return (
+        new_columns, jnp.transpose(coefficients, (1, 2, 0)), hessenberg,
+        jnp.transpose(gram, (0, 2, 1, 3)), new_images,
+    )
 
 
 def solution(mesh):

time: 115 us -> 110 us (0.957)
  local copies, waits for them, and re-layouts: 5.84 us -> 2.35 us
  Pallas kernels: 109 us -> 106 us
    unnamed x12 -> x6, local copies, waits for them, and re-layouts: 5.64 us -> 2.35 us
    pallas_call x1 -> x2, Pallas kernels: 109 us -> 106 us  [the longest x1 105 us: local(): pl.pallas_call(functools.partial(kernel, sizes), out_shape=shapes, in_spe...]
where the time goes in v2:
time: 110 us; the launch traced here: 109 us
  Pallas kernels  106 us (96%)
  local copies, waits for them, and re-layouts  2.35 us (2%)
    pallas_call x1, Pallas kernels, local(): pl.pallas_call(functools.partial(kernel, sizes), out_shape=shapes, in_spe...  105 us
    unnamed x6, local copies, waits for them, and re-layouts  2.35 us

profile of v2, /device:TPU:2, one launch (start us, length us, event | category | flops | bytes accessed | tf_op | source)
XLA Modules:
  0.0 109.4 jit_solution(4047343349884572675)
XLA Ops:
  0.6 0.0 copy-start
  0.6 0.9 copy-done
  1.5 0.0 copy-start.1
  1.5 0.7 copy-done.1
  2.3 0.0 copy-start.2
  2.3 0.7 copy-done.2
  3.0 105.4 %shard_map.83 = (f32[3,48,128]{2,1,0:T(8,128)S(1)}, f32[37,4,40]{2,1,0:T(4,128)S(1)}, f32[3,37]{1,0:T(4,128)S(1)}, f32[5,5,40,40]{3,2,1,0:T(8,128)S(1)}, f32[3,48,128]{2,1,0:T(8,128)S(1)}) custom-call(f32[1776,128]{1,0:T(8,128)} %bitcast.5, f32[34,4,37]{2,1,0:T(4,128)S(1)} %bitcast.4, f32[48,128]{1,0:T(8,128)S(1)} %copy-done.1, f32[48,128]{1,0:T(8,128)S(1)} %copy-done.2), custom_call_target="tpu_custom_call" | custom-call | tf_op jit(solution)/shard_map/pallas_call | solution.py:787
  108.4 0.9 shard_map.84
Async XLA Ops:
  0.6 0.9 copy-start
  1.5 0.7 copy-start.1
  2.3 0.7 copy-start.2

commit v3 on v2

--- a/solution.py
+++ b/solution.py
@@ -30,6 +30,7 @@
 GROUP = 8
 FIRST = 128
 SECOND = 192
+CENTRE = pl.ds(GHOST * LANES, ROWS * LANES)
 F32 = jnp.float32
 
 
@@ -120,13 +121,13 @@
 
 
 def kernel(
-    sizes, x_hbm, kr_hbm, st_hbm, ro_hbm,
+    sizes, x_hbm, small_ref,
     newc_ref, coef_ref, hess_ref, gram_ref, newi_ref,
-    x_ref, kr_ref, st_ref, ro_ref, in_sem,
-    X, SD, CF, PL, PR, RRB, RLB, AHL, ACC, AC0, BIG, FULL, BIG2, FULL2, GS, GC, LB, GB0, CB, MT, HS, KS,
+    x_ref, in_sem,
+    X, SD, CF, PL, PR, RRB, RLB, AHL, ACC, AC0, BIG, FULL, BIG2, FULL2, GS, GC, LB, GB0, CB, MT, HS,
     U0, PK, HT, HB, KRB, KLB, VB, VW, UV, DN,
-    slots_big, slots_two, slots_small, slots_last, slots_late,
-    hsend, hrecv, bsend, brecv, csend, crecv, usend, urecv, ssend, srecv, lsend, lrecv,
+    slots_big, slots_two, slots_small, slots_last, slots_late, slots_early,
+    hsend, hrecv, bsend, brecv, csend, crecv, usend, urecv, ssend, srecv, lsend, lrecv, esend, erecv,
 ):
     nrow = sizes["x"] * sizes["core"]
     ncol = sizes["y"] * sizes["z"]
@@ -137,14 +138,8 @@
     stage_offsets = [offsets(sizes, axes) for axes in STAGES]
     pending = []
 
-    loads = [
-        pltpu.make_async_copy(src, dst, in_sem.at[i])
-        for i, (src, dst) in enumerate(
-            ((x_hbm, x_ref), (st_hbm, st_ref), (ro_hbm, ro_ref), (kr_hbm, kr_ref))
-        )
-    ]
-    for copy in loads:
-        copy.start()
+    load = pltpu.make_async_copy(x_hbm, x_ref, in_sem.at[0])
+    load.start()
 
     barrier = pltpu.get_barrier_semaphore()
     count = 0
@@ -176,13 +171,12 @@
             r = 4 * i + k
             at = pl.multiple_of((r + GHOST) * K, 8)
             X[0][pl.ds(at, R), :] = x_ref[pl.ds(r, R, stride=ROWS), :]
-            X[0][pl.ds(at + R, 1), :] = st_ref[pl.ds(r, 1), :]
-            X[0][pl.ds(at + R + 1, 1), :] = ro_ref[pl.ds(r, 1), :]
+            X[0][pl.ds(at + R, 1), :] = small_ref[pl.ds(r, 1), :]
+            X[0][pl.ds(at + R + 1, 1), :] = small_ref[pl.ds(ROWS + r, 1), :]
             X[0][pl.ds(at + R + 2, 1), :] = jnp.zeros((1, LANES), F32)
         return carry
 
-    for copy in loads[:3]:
-        copy.wait()
+    load.wait()
     lax.fori_loop(0, ROWS // 4, load_rows, 0)
     lane_k = iota((K, LANES), 1)
 
@@ -220,11 +214,42 @@
         send(PR.at[1], RLB.at[0], hsend.at[7], hrecv.at[7], near(sizes, 1, 1)),
     ]
 
-    loads[3].wait()
-    KS[...] = jnp.zeros((K, 256), F32)
+    class Sum:
+        def __init__(self, boxes, send_sems, recv_sems):
+            self.boxes, self.send_sems, self.recv_sems, self.sem = boxes, send_sems, recv_sems, 0
+
+        def start(self, stage, value):
+            me = place(sizes, STAGES[stage])
+            box = self.boxes[stage]
+            box[me] = value
+            self.copies = []
+            for off in stage_offsets[stage]:
+                to = peer_of(sizes, STAGES[stage], off)
+                sems = self.send_sems.at[self.sem], self.recv_sems.at[self.sem]
+                self.copies.append(send(box.at[me], box.at[me], *sems, to))
+                self.sem += 1
+
+        def finish(self, stage):
+            for copy in self.copies:
+                copy.wait_recv()
+            box = self.boxes[stage]
+            total = box[0]
+            for i in range(1, len(stage_offsets[stage]) + 1):
+                total = total + box[i]
+            return total
+
+    early = Sum(slots_early, esend, erecv)
+    raw_lines = jnp.concatenate([X[0][line(r + GHOST), :] for r in range(ROWS)], axis=1)
+    raw_part = jnp.concatenate([dot3(raw_lines, raw_lines, 1, 1), jnp.zeros((K, LANES - K), F32)], axis=1)
+    early.start(0, raw_part)
+
+    blank_half = jnp.zeros((KRYLOV, LANES), F32)
+    pt = jnp.zeros((KRYLOV, 256), F32)
     for j in range(4):
-        KS[pl.ds(0, KRYLOV), pl.ds(j * K, R)] = kr_ref[:, j, :]
-    pt = KS[...]
+        v = small_ref[pl.ds(2 * ROWS + j, KRYLOV, stride=4), :]
+        v = jnp.concatenate([v, blank_half], axis=1)
+        pt = pt + (pltpu.roll(v, j * K, 1) if j else v)
+    pt = jnp.concatenate([pt, jnp.zeros((K - KRYLOV, 256), F32)], axis=0)
     kgram = dot(pt, pt, 1, 1)
     kgram = jnp.concatenate([kgram, jnp.zeros((K, LANES - K), F32)], axis=1)
     kinv = forward_inverse(augmented(kgram, 0.0, KRYLOV), KRYLOV)
@@ -236,6 +261,7 @@
     BIG[...] = jnp.zeros((FIRST, LANES), F32)
     BIG2[...] = jnp.zeros((SECOND, LANES), F32)
     CF[...] = jnp.zeros((10, 64, LANES), F32)
+    AHL[pl.ds(PADDED, 256 - PADDED), :] = jnp.zeros((256 - PADDED, (ROWS + 8) * LANES), jnp.bfloat16)
     VW[...] = jnp.zeros((ROWS * 8, LANES), F32)
     UV[...] = jnp.zeros((ROWS * 24, LANES), F32)
 
@@ -287,6 +313,11 @@
     order_zero(36, 16, 2, 0)
     order_zero(52, 4, 3, 0)
 
+    def split_tile(t, at, a):
+        hi = a.astype(jnp.bfloat16)
+        AHL[pl.ds(16 * t, 16), at] = hi
+        AHL[pl.ds(256 + 16 * t, 16), at] = (a - hi.astype(F32)).astype(jnp.bfloat16)
+
     def images(m, n):
         def body(b, carry):
             mids, sides = [], []
@@ -316,51 +347,39 @@
                 X[m][line(rho), :] = mids[k]
                 if m < 4:
                     SD[m][line(rho), :] = sides[k]
+                at = pl.ds(pl.multiple_of(rho * LANES, LANES), LANES)
+                new = mids[k]
+                if m in (1, 3):
+                    ends = jnp.concatenate([X[m - 1][pl.ds(pl.multiple_of(rho * K + 32, 8), 8), :], new[0:8, :]], axis=0)
+                    split_tile(5 * (m - 1) // 2 + 2, at, ends)
+                    split_tile(5 * (m - 1) // 2 + 3, at, new[8:24, :])
+                    split_tile(5 * (m - 1) // 2 + 4, at, new[24:40, :])
+                else:
+                    split_tile(5 * m // 2, at, new[0:16, :])
+                    split_tile(5 * m // 2 + 1, at, new[16:32, :])
+                if m == 4:
+                    split_tile(12, at, jnp.concatenate([new[32:40, :], jnp.zeros((8, LANES), F32)], axis=0))
+                if m == 1:
+                    old = X[0][pl.ds(pl.multiple_of(rho * K, 8), 32), :]
+                    split_tile(0, at, old[0:16, :])
+                    split_tile(1, at, old[16:32, :])
             return carry
 
         lax.fori_loop(0, (ROWS + 8 - 2 * m) // n, body, 0)
 
-    for m, n in zip(range(1, ORDERS), (6, 4, 5, 6)):
+    for m, n in zip(range(1, ORDERS), (3, 4, 5, 6)):
         images(m, n)
-
-    AC0[...] = jnp.zeros((96, 512), F32)
-    AHL[pl.ds(PADDED, 256 - PADDED), :] = jnp.zeros((256 - PADDED, ROWS * LANES), jnp.bfloat16)
-
-    def lines(first, n):
-        blank = [jnp.zeros((PADDED - FIELDS, LANES), F32)]
-        return jnp.concatenate(
-            [
-                jnp.concatenate([X[m][line(first + k + GHOST), :] for m in range(ORDERS)] + blank, axis=0)
-                for k in range(n)
-            ],
-            axis=1,
-        )
+        if m == 2:
+            early.start(1, early.finish(0))
+        if m == 4:
+            early.start(2, early.finish(1))
+
 
     def bdot(a, b):
         return lax.dot_general(a, b, (((1,), (1,)), ((), ())), preferred_element_type=F32)
 
-    def split_rows(g):
-        for part in range(GROUP // 2):
-            a = lines(GROUP * g + 2 * part, 2)
-            hi = a.astype(jnp.bfloat16)
-            at = pl.ds(pl.multiple_of((GROUP * g + 2 * part) * LANES, LANES), 2 * LANES)
-            AHL[pl.ds(0, PADDED), at] = hi
-            AHL[pl.ds(256, PADDED), at] = (a - hi.astype(F32)).astype(jnp.bfloat16)
-
-    def gram_rows(g):
-        at = pl.ds(pl.multiple_of(GROUP * g * LANES, LANES), GROUP * LANES)
-        first = jnp.concatenate([AHL[pl.ds(0, 48), at], AHL[pl.ds(256, 48), at]], axis=0)
-        return bdot(first, AHL[:, at])
-
-    def gram_step(g, carry):
-        part = gram_rows(g - 1)
-        split_rows(g)
-        AC0[:, pl.ds(0, 256 + PADDED)] += part
-        return carry
-
-    split_rows(0)
-    lax.fori_loop(1, ROWS // GROUP, gram_step, 0)
-    AC0[:, pl.ds(0, 256 + PADDED)] += gram_rows(ROWS // GROUP - 1)
+    first_rows = jnp.concatenate([AHL[pl.ds(0, 48), CENTRE], AHL[pl.ds(256, 48), CENTRE]], axis=0)
+    AC0[:, pl.ds(0, 256 + PADDED)] = bdot(first_rows, AHL[:, CENTRE])
     top = AC0[pl.ds(0, K), pl.ds(0, 256)] + AC0[pl.ds(48, K), pl.ds(0, 256)] + AC0[pl.ds(0, K), pl.ds(256, 256)]
     lane_w = iota((K, 256), 1)
     top = jnp.where(lane_w < FIELDS, top, 0.0)
@@ -412,30 +431,6 @@
             for off in stage_offsets[0]:
                 self.emit(self.whole.at[self.own], self.whole.at[self.own], peer_of(sizes, ROW, off))
 
-    class Sum:
-        def __init__(self, boxes, send_sems, recv_sems):
-            self.boxes, self.send_sems, self.recv_sems, self.sem = boxes, send_sems, recv_sems, 0
-
-        def start(self, stage, value):
-            me = place(sizes, STAGES[stage])
-            box = self.boxes[stage]
-            box[me] = value
-            self.copies = []
-            for off in stage_offsets[stage]:
-                to = peer_of(sizes, STAGES[stage], off)
-                sems = self.send_sems.at[self.sem], self.recv_sems.at[self.sem]
-                self.copies.append(send(box.at[me], box.at[me], *sems, to))
-                self.sem += 1
-
-        def finish(self, stage):
-            for copy in self.copies:
-                copy.wait_recv()
-            box = self.boxes[stage]
-            total = box[0]
-            for i in range(1, len(stage_offsets[stage]) + 1):
-                total = total + box[i]
-            return total
-
     one = Reduction(BIG, FULL, slots_big, FIRST, bsend, brecv)
     two = Reduction(BIG2, FULL2, slots_two, SECOND, csend, crecv)
     one.start(0)
@@ -443,7 +438,7 @@
     ACC[...] = jnp.zeros((256 + PADDED, 256), F32)
 
     def gram_rest(g, carry):
-        at = pl.ds(pl.multiple_of(GROUP * g * LANES, LANES), GROUP * LANES)
+        at = pl.ds(pl.multiple_of((GHOST + GROUP * g) * LANES, LANES), GROUP * LANES)
         ACC[:, pl.ds(0, PADDED)] += bdot(AHL[:, at], AHL[pl.ds(0, PADDED), at])
         return carry
 
@@ -460,10 +455,17 @@
     BIG2[pl.ds(2 * K, K), :] = jnp.where(lane_n >= 80, strip(4, -80), strip(3, -120))
     BIG2[pl.ds(3 * K, K), :] = strip(1, -160)
 
+    raw_gram = early.finish(2) * inverse_total
     for stage in range(3):
         one.finish(stage)
         if stage < 2:
             one.start(stage + 1)
+        if stage == 0:
+            finv = forward_inverse(augmented(raw_gram, GRAM_SHIFT, R), R)
+            finv = jnp.where(sub_k < R, finv, 0.0)
+            finv_wide = jnp.concatenate([finv, jnp.zeros((K, LANES), F32)], axis=1)
+            for a in range(ORDERS):
+                LB[pl.ds(a * K, K), :] = pltpu.roll(finv_wide, a * K, 1) if a else finv_wide
     one.gather()
     one.arrived()
     two.start(0)
@@ -490,11 +492,6 @@
                 lane_w >= a * K, GS[pl.ds(a * K, K), :], mirrored[a * K : (a + 1) * K, :]
             )
 
-    finv = forward_inverse(augmented(GS[pl.ds(0, K), pl.ds(0, LANES)], GRAM_SHIFT, R), R)
-    finv = jnp.where(sub_k < R, finv, 0.0)
-    finv_wide = jnp.concatenate([finv, jnp.zeros((K, LANES), F32)], axis=1)
-    for a in range(ORDERS):
-        LB[pl.ds(a * K, K), :] = pltpu.roll(finv_wide, a * K, 1) if a else finv_wide
     square = (iota((LANES, LANES), 0) < K) & (iota((LANES, LANES), 1) < K)
     small = jnp.where(square, LB[pl.ds(0, LANES), pl.ds(0, LANES)], 0.0)
     GB0[...] = dot3(dot3(LB[...], GC[...], 1, 0), small, 1, 1)
@@ -509,13 +506,13 @@
         return jnp.concatenate([v_hi, v - v_hi], axis=0).astype(jnp.bfloat16)
 
     def with_old(v):
-        old = bdot(v, AHL[...])
+        old = bdot(v, AHL[:, CENTRE])
         old = old[0:8, :] + old[8:16, :]
         d = old[:, 0:256] + jnp.concatenate([old[:, 256:], jnp.zeros((8, 256 - PADDED), F32)], axis=1)
         return jnp.where(lane8 < FIELDS, d, 0.0)
 
     def with_first(v):
-        first = jnp.concatenate([AHL[pl.ds(0, 48), :], AHL[pl.ds(256, 48), :]], axis=0)
+        first = jnp.concatenate([AHL[pl.ds(0, 48), CENTRE], AHL[pl.ds(256, 48), CENTRE]], axis=0)
         part = bdot(v, first)
         return part[0:8, 0:K] + part[8:16, 0:K] + part[0:8, 48 : 48 + K]
 
@@ -759,14 +756,14 @@
     half = lambda *shape: pltpu.VMEM(shape, jnp.bfloat16)
     dma = lambda *shape: pltpu.SemaphoreType.DMA(shape)
     scratch = [
-        vmem(R * ROWS, LANES), vmem(KRYLOV, 4, R), vmem(ROWS, LANES), vmem(ROWS, LANES), dma(4),
+        vmem(R * ROWS, LANES), dma(1),
         [vmem((ROWS + 8) * K, LANES) for _ in range(ORDERS)],
         [vmem((ROWS + 8) * K, LANES) for _ in range(ORDERS - 1)],
         vmem(10, 64, LANES), vmem(2, K, LANES), vmem(2, K, LANES), vmem(4, K, LANES), vmem(4, K, LANES),
-        half(256 + PADDED, ROWS * LANES), vmem(256 + PADDED, 256), vmem(96, 512),
+        half(256 + PADDED, (ROWS + 8) * LANES), vmem(256 + PADDED, 256), vmem(96, 512),
         vmem(FIRST, LANES), vmem(FIRST, LANES), vmem(SECOND, LANES), vmem(SECOND, LANES),
         vmem(256, 256), vmem(256, LANES), vmem(256, 256),
-        vmem(256, LANES), vmem(FIELDS + 24, LANES), vmem(LANES, 256), vmem(LANES, LANES), vmem(K, 256),
+        vmem(256, LANES), vmem(FIELDS + 24, LANES), vmem(LANES, 256), vmem(LANES, LANES),
         vmem(STEPS, ROWS, LANES), vmem(STEPS, 8, LANES), vmem(STEPS, 8, LANES), vmem(STEPS, 8, LANES),
         vmem(STEPS, 3, 8, LANES), vmem(STEPS, 3, 8, LANES), vmem(ORDERS, ROWS, LANES),
         vmem(ROWS * 8, LANES), vmem(ROWS * 24, LANES), vmem(8, 256),
@@ -775,27 +772,31 @@
         [vmem(STEPS - 1, n, 8, LANES) for n in counts],
         [vmem(n, 8, 256) for n in counts],
         [vmem(STEPS - 1, n, 8, 256) for n in counts],
+        [vmem(n, K, LANES) for n in counts],
         dma(8), dma(8), dma(big_copies), dma(big_copies), dma(big_copies), dma(big_copies),
         dma(STEPS, 8), dma(STEPS, 8), dma(STEPS, small_copies), dma(STEPS, small_copies),
         dma(STEPS - 1, small_copies), dma(STEPS - 1, small_copies),
+        dma(small_copies), dma(small_copies),
     ]
     shape = lambda *dims: jax.ShapeDtypeStruct(dims, F32)
     shapes = [
         shape(STEPS, ROWS, LANES), shape(width, 4, K), shape(STEPS, width),
         shape(ORDERS, ORDERS, K, K), shape(STEPS, ROWS, LANES),
     ]
+    krylov_lines = jnp.transpose(krylov_raw, (2, 0, 1)).reshape(4 * KRYLOV, R)
+    krylov_lines = jnp.pad(krylov_lines, ((0, 0), (0, LANES - R)))
+    small = jnp.concatenate([stiffness, rotation, krylov_lines], axis=0)
     results = pl.pallas_call(
         functools.partial(kernel, sizes),
         out_shape=shapes,
-        in_specs=[pl.BlockSpec(memory_space=pltpu.HBM)] * 4,
+        in_specs=[pl.BlockSpec(memory_space=pltpu.HBM), pl.BlockSpec(memory_space=pltpu.VMEM)],
         out_specs=[pl.BlockSpec(memory_space=pltpu.VMEM)] * 5,
         scratch_shapes=scratch,
         compiler_params=pltpu.CompilerParams(
             collective_id=0, has_side_effects=True, vmem_limit_bytes=55_000_000
         ),
     )(
-        basis_raw.reshape(R * ROWS, LANES), jnp.transpose(krylov_raw, (2, 0, 1)),
-        stiffness, rotation,
+        basis_raw.reshape(R * ROWS, LANES), small,
     )
     new_columns, coefficients, hessenberg, gram, new_images = pl.pallas_call(
         handed_out,

time: 110 us -> 108 us (0.982)
  local copies, waits for them, and re-layouts: 2.35 us -> 0 us
    unnamed x6 -> x0, local copies, waits for them, and re-layouts: 2.35 us -> none
where the time goes in v3:
time: 108 us
  Pallas kernels  106 us (98%)
    pallas_call x1, Pallas kernels, local(): pl.pallas_call(functools.partial(kernel, sizes), out_shape=shapes, in_spe...  105 us

profile of v3, /device:TPU:2, one launch (start us, length us, event | category | flops | bytes accessed | tf_op | source)
XLA Modules:
  0.0 108.0 jit_solution(5419540883486115722)
XLA Ops:
  0.6 0.9 select_maximum_fusion.small_ref
  1.5 105.4 %shard_map.83 = (f32[3,48,128]{2,1,0:T(8,128)S(1)}, f32[37,4,40]{2,1,0:T(4,128)S(1)}, f32[3,37]{1,0:T(4,128)S(1)}, f32[5,5,40,40]{3,2,1,0:T(8,128)S(1)}, f32[3,48,128]{2,1,0:T(8,128)S(1)}) custom-call(f32[1776,128]{1,0:T(8,128)} %bitcast.6, f32[232,128]{1,0:T(8,128)S(1)} %select_maximum_fusion.small_ref), custom_call_target="tpu_custom_call" | custom-call | tf_op jit(solution)/shard_map/pallas_call | solution.py:789
  106.9 0.9 shard_map.84

commit v4 on v3

--- a/solution.py
+++ b/solution.py
@@ -28,7 +28,7 @@
 GHOST = 4
 PADDED = 208
 GROUP = 8
-FIRST = 128
+FIRST = 64
 SECOND = 192
 CENTRE = pl.ds(GHOST * LANES, ROWS * LANES)
 F32 = jnp.float32
@@ -186,8 +186,8 @@
     def pack(base, n, q):
         def body(b, carry):
             left, right = carry
-            for k in range(8):
-                i = 8 * b + k
+            for k in range(16):
+                i = 16 * b + k
                 row = X[0][line(base + i), :]
                 here = (lane_k >= 4 * i) & (lane_k < 4 * i + 4)
                 left = jnp.where(here, pltpu.roll(row, 4 * i, 1), left)
@@ -195,7 +195,7 @@
             return left, right
 
         zero = jnp.zeros((K, LANES), F32)
-        left, right = lax.fori_loop(0, n // 8, body, (zero, zero))
+        left, right = lax.fori_loop(0, n // 16, body, (zero, zero))
         PL[q, :, :] = left
         PR[q, :, :] = right
 
@@ -278,10 +278,12 @@
     sub_k = iota((K, LANES), 0)
 
     def order_zero(base, n, part, first):
+        unroll = min(n, 16)
+
         def body(b, carry):
             stores = []
-            for k in range(4):
-                i = 4 * b + k
+            for k in range(unroll):
+                i = unroll * b + k
                 rho = base + i
                 g = my_row * ROWS + rho - GHOST
                 row_mask = ((g >= 0) & (g < grid_rows)).astype(F32)
@@ -306,7 +308,7 @@
                 SD[0][line(rho), :] = jnp.where(sub_k < R, side[0], 0.0)
             return carry
 
-        lax.fori_loop(0, n // 4, body, 0)
+        lax.fori_loop(0, n // unroll, body, 0)
 
     order_zero(0, 4, 0, 12)
     order_zero(4, 32, 1, 0)
@@ -367,11 +369,11 @@
 
         lax.fori_loop(0, (ROWS + 8 - 2 * m) // n, body, 0)
 
-    for m, n in zip(range(1, ORDERS), (3, 4, 5, 6)):
+    for m, n in zip(range(1, ORDERS), (18, 26, 25, 24)):
         images(m, n)
-        if m == 2:
+        if m == 1:
             early.start(1, early.finish(0))
-        if m == 4:
+        if m == 3:
             early.start(2, early.finish(1))
 
 
@@ -383,8 +385,14 @@
     top = AC0[pl.ds(0, K), pl.ds(0, 256)] + AC0[pl.ds(48, K), pl.ds(0, 256)] + AC0[pl.ds(0, K), pl.ds(256, 256)]
     lane_w = iota((K, 256), 1)
     top = jnp.where(lane_w < FIELDS, top, 0.0)
-    BIG[pl.ds(0, K), :] = top[:, 0:LANES]
-    BIG[pl.ds(K, K), :] = top[:, LANES:]
+    BIG[pl.ds(0, K), :] = pltpu.roll(top, 256 - K, 1)[:, 0:LANES]
+    tail = pltpu.roll(top, 256 - 168, 1)[:, 0:LANES]
+    quarter = iota((8, LANES), 1) // 32
+    mixed = tail[0:8, :]
+    for t in range(1, 4):
+        mixed = jnp.where(quarter == t, pltpu.roll(tail[8 * t : 8 * t + 8, :], 32 * t, 1), mixed)
+    BIG[pl.ds(K, 8), :] = mixed
+    BIG[pl.ds(K + 8, 8), :] = tail[32:40, :]
 
     class Reduction:
         def __init__(self, big, whole, boxes, total_rows, send_sems, recv_sems):
@@ -455,12 +463,12 @@
     BIG2[pl.ds(2 * K, K), :] = jnp.where(lane_n >= 80, strip(4, -80), strip(3, -120))
     BIG2[pl.ds(3 * K, K), :] = strip(1, -160)
 
-    raw_gram = early.finish(2) * inverse_total
     for stage in range(3):
         one.finish(stage)
         if stage < 2:
             one.start(stage + 1)
         if stage == 0:
+            raw_gram = early.finish(2) * inverse_total
             finv = forward_inverse(augmented(raw_gram, GRAM_SHIFT, R), R)
             finv = jnp.where(sub_k < R, finv, 0.0)
             finv_wide = jnp.concatenate([finv, jnp.zeros((K, LANES), F32)], axis=1)
@@ -470,8 +478,18 @@
     one.arrived()
     two.start(0)
 
-    GS[pl.ds(0, K), pl.ds(0, LANES)] = FULL[pl.ds(0, K), :]
-    GS[pl.ds(0, K), pl.ds(LANES, LANES)] = FULL[pl.ds(K, K), :]
+    mixed = FULL[pl.ds(K, 8), :]
+    tail = jnp.concatenate(
+        [pltpu.roll(mixed, LANES - 32 * t, 1) if t else mixed for t in range(4)] + [FULL[pl.ds(K + 8, 8), :]],
+        axis=0,
+    )
+    blank = jnp.zeros((K, LANES), F32)
+    body = pltpu.roll(jnp.concatenate([FULL[pl.ds(0, K), :], blank], axis=1), K, 1)
+    tail = pltpu.roll(jnp.concatenate([tail, blank], axis=1), 168, 1)
+    head = jnp.concatenate([jnp.where((sub_k < R) & (lane_k < R), raw_gram, 0.0), blank], axis=1)
+    GS[pl.ds(0, K), :] = jnp.where(
+        lane_w < K, head, jnp.where(lane_w < 168, body, jnp.where(lane_w < FIELDS, tail, 0.0))
+    )
     GC[...] = jnp.transpose(GS[pl.ds(0, LANES), :])
 
     def assemble_rest():
@@ -667,17 +685,19 @@
             total_sum.start(stage, value)
             if stage == 0 and s + 1 < STEPS:
                 rest = jnp.where((lane8 >= K) & (sub8 >= 1) & (sub8 < ORDERS), with_old(v), 0.0)
-            if s == 0 and stage == 2:
+            if s == 0 and stage == 0:
                 two.finish(1)
                 two.start(2)
+            if s == 0 and stage == 2:
                 late[0].start(0, rest)
             if s == 1 and stage == 0:
                 two.arrived()
                 assemble_rest()
+            if s == 1 and stage == 0:
+                late[0].start(2, late[0].finish(1))
             if s == 1 and stage == 2:
-                late[0].start(2, late[0].finish(1))
                 late[1].start(0, rest)
-            if s == 2 and stage == 2:
+            if s == 2 and stage == 0:
                 late[1].start(2, late[1].finish(1))
             value = total_sum.finish(stage)
         if s + 1 < STEPS:

time: 108 us -> 103 us (0.954)
  Pallas kernels: 106 us -> 101 us
    pallas_call x1, Pallas kernels: 105 us -> 100 us  [local(): pl.pallas_call(functools.partial(kernel, sizes), out_shape=shapes, in_spe...]
where the time goes in v4:
time: 103 us
  Pallas kernels  101 us (98%)
    pallas_call x1, Pallas kernels, local(): pl.pallas_call(functools.partial(kernel, sizes), out_shape=shapes, in_spe...  100 us

profile of v4, /device:TPU:2, one launch (start us, length us, event | category | flops | bytes accessed | tf_op | source)
XLA Modules:
  0.0 102.7 jit_solution(6193363904804700147)
XLA Ops:
  0.6 0.9 select_maximum_fusion.small_ref
  1.5 100.1 %shard_map.83 = (f32[3,48,128]{2,1,0:T(8,128)S(1)}, f32[37,4,40]{2,1,0:T(4,128)S(1)}, f32[3,37]{1,0:T(4,128)S(1)}, f32[5,5,40,40]{3,2,1,0:T(8,128)S(1)}, f32[3,48,128]{2,1,0:T(8,128)S(1)}) custom-call(f32[1776,128]{1,0:T(8,128)} %bitcast.6, f32[232,128]{1,0:T(8,128)S(1)} %select_maximum_fusion.small_ref), custom_call_target="tpu_custom_call" | custom-call | tf_op jit(solution)/shard_map/pallas_call | solution.py:809
  101.6 0.9 shard_map.84

commit v5 on v4

--- a/solution.py
+++ b/solution.py
@@ -138,7 +138,7 @@
     stage_offsets = [offsets(sizes, axes) for axes in STAGES]
     pending = []
 
-    load = pltpu.make_async_copy(x_hbm, x_ref, in_sem.at[0])
+    load = pltpu.make_async_copy(x_hbm, x_ref.at[pl.ds(0, R * ROWS)], in_sem.at[0])
     load.start()
 
     barrier = pltpu.get_barrier_semaphore()
@@ -776,7 +776,7 @@
     half = lambda *shape: pltpu.VMEM(shape, jnp.bfloat16)
     dma = lambda *shape: pltpu.SemaphoreType.DMA(shape)
     scratch = [
-        vmem(R * ROWS, LANES), dma(1),
+        vmem(K * ROWS, LANES), dma(1),
         [vmem((ROWS + 8) * K, LANES) for _ in range(ORDERS)],
         [vmem((ROWS + 8) * K, LANES) for _ in range(ORDERS - 1)],
         vmem(10, 64, LANES), vmem(2, K, LANES), vmem(2, K, LANES), vmem(4, K, LANES), vmem(4, K, LANES),
@@ -804,7 +804,7 @@
         shape(ORDERS, ORDERS, K, K), shape(STEPS, ROWS, LANES),
     ]
     krylov_lines = jnp.transpose(krylov_raw, (2, 0, 1)).reshape(4 * KRYLOV, R)
-    krylov_lines = jnp.pad(krylov_lines, ((0, 0), (0, LANES - R)))
+    krylov_lines = jnp.pad(krylov_lines, ((0, 24), (0, LANES - R)))
     small = jnp.concatenate([stiffness, rotation, krylov_lines], axis=0)
     results = pl.pallas_call(
         functools.partial(kernel, sizes),

time: 103 us -> 103 us (level)
  no operation moved by 1% of the time
where the time goes in v5:
time: 103 us
  Pallas kernels  101 us (98%)
    pallas_call x1, Pallas kernels, local(): pl.pallas_call(functools.partial(kernel, sizes), out_shape=shapes, in_spe...  99.9 us

profile of v5, /device:TPU:2, one launch (start us, length us, event | category | flops | bytes accessed | tf_op | source)
XLA Modules:
  0.0 102.5 jit_solution(996932929998161441)
XLA Ops:
  0.6 0.9 select_maximum_fusion.small_ref
  1.5 99.9 %shard_map.83 = (f32[3,48,128]{2,1,0:T(8,128)S(1)}, f32[37,4,40]{2,1,0:T(4,128)S(1)}, f32[3,37]{1,0:T(4,128)S(1)}, f32[5,5,40,40]{3,2,1,0:T(8,128)S(1)}, f32[3,48,128]{2,1,0:T(8,128)S(1)}) custom-call(f32[1776,128]{1,0:T(8,128)} %bitcast.6, f32[256,128]{1,0:T(8,128)S(1)} %select_maximum_fusion.small_ref), custom_call_target="tpu_custom_call" | custom-call | tf_op jit(solution)/shard_map/pallas_call | solution.py:809
  101.5 0.9 shard_map.84
